TPU v7x, 512 devices: a whole 4x4x16 slice. The times are simulated.
512 devices in a mesh: clump: 128 (over z, y, core), grp: 4 (over x).
Axes of the slice: x: 4, y: 4, z: 16, core: 2. Of those that a mesh axis runs over, the one named last changes fastest.
Arguments:
- flux: float32 [512, 1024, 64], P(('clump', 'grp')), may hold values from -6 to 6
- patch_pft: int32 [512, 1024], P(('clump', 'grp')), may hold values from 0 to 15
- patch_wt: float32 [512, 1024], P(('clump', 'grp')), may hold values from 0.2 to 2
- patch_col: int32 [512, 1024], P(('clump', 'grp')), may hold values from 0 to 511, never falling along the last dimension, each value on 1 to 4 neighbouring positions
- col_wt: float32 [512, 512], P(('clump', 'grp')), may hold values from 0.2 to 2
- col_lu: int32 [512, 512], P(('clump', 'grp')), may hold values from 0 to 255, never falling along the last dimension, each value on 1 to 4 neighbouring positions
- lu_wt: float32 [512, 256], P(('clump', 'grp')), may hold values from 0.2 to 2
- lu_grid: int32 [512, 256], P(('clump', 'grp')), may hold values from 0 to 127, never falling along the last dimension, each value on 1 to 4 neighbouring positions
- cell_target: int32 [512, 128], P(('clump', 'grp')), may hold values from 0 to 65535, as said below
- patch_count: int32 [512], P(('clump', 'grp')), may hold values from 64 to 1024
- pft_scale: float32 [16, 64], replicated, may hold values from 0.3 to 3
- cpl_frac: float32 [65536], P(('clump', 'grp')), may hold values from 0.2 to 0.9
- cpl_field: float32 [65536, 64], P(('clump', 'grp')), may hold values from -6 to 6
Outputs:
- grid_merged: float32 [65536, 64], P(('clump', 'grp'))
- anomaly: float32 [512, 1024, 64], P(('clump', 'grp'))
Inputs may be any that keep to these rules, and one draw needn't show every extreme that they name: `patch_col`: within each device's row the column numbers never fall, and each column holds 1 to 4 patch slots. `col_lu`: within each device's row the landunit numbers never fall, and each landunit holds 1 to 4 columns. `lu_grid`: within each device's row the gridcell numbers never fall, and each gridcell holds 1 to 4 landunits. `cell_target`: all devices' entries together are a permutation of 0 to 65535; the coupler owner of an entry q is q // 128, and each device's 128 gridcells go to 64 owners, exactly 2 to each.
All inputs are finite; a program needn't handle non-finite values.
Results may differ from a plain program's by a relative error of at most 0.0003.
Values sent between devices are 32-bit elements; how exact they have to be, the bound alone decides.
No kernel may reach another device: no remote copies, remote signals or barrier semaphores. Data moves between devices by JAX's collectives and lax.ppermute only.
A program may use at most 64 MiB of HBM per device.

v0:
```python
import jax
import jax.numpy as jnp
from jax import lax
from jax.sharding import PartitionSpec as P

HIGH = lax.Precision.HIGHEST


def split_up(x, dim, length):
    shape = x.shape
    parts = x.reshape(*shape[:dim], length, shape[dim] // length, *shape[dim + 1 :])
    return jnp.moveaxis(parts, dim, 0)


def laid_out(parts, dim):
    shape = list(parts.shape[1:])
    shape[dim] *= parts.shape[0]
    return jnp.moveaxis(parts, 0, dim).reshape(shape)


def exchange_both(x, axis, axes, splits, concats):
    sizes = [lax.axis_size(a) for a in axes]
    parts = split_up(x, splits[0], sizes[0])
    parts = jnp.moveaxis(split_up(parts, splits[1] + 1, sizes[1]), 0, 1)
    inside = parts.shape[2:]
    parts = parts.reshape(-1, *inside)
    parts = lax.all_to_all(parts, axis, split_axis=0, concat_axis=0, tiled=True)
    parts = laid_out(parts.reshape(*sizes, *inside), concats[0] + 1)
    return laid_out(parts, concats[1])


def window_pick(padded, start, relative, width):
    window = lax.dynamic_slice_in_dim(padded, start, width, 0)
    onehot = (relative[:, None] == jnp.arange(width, dtype=jnp.int32)[None, :]).astype(jnp.float32)
    return jnp.dot(onehot, window, precision=HIGH)


def per_device(
    flux,
    patch_pft,
    patch_wt,
    patch_col,
    col_wt,
    col_lu,
    lu_wt,
    lu_grid,
    cell_target,
    patch_count,
    pft_scale,
    cpl_frac,
    cpl_field,
):
    n_clump = lax.axis_size("clump")
    n_group = lax.axis_size("grp")
    n_devices = n_clump * n_group
    values = flux[0]
    patches = values.shape[0]
    width_vars = values.shape[1]
    cell_count = cell_target.shape[1]
    capacity = max(2, 2 * cell_count // n_devices)
    slot_total = n_devices * capacity
    block = min(512, patches)
    blocks = patches // block
    position = jnp.arange(patches, dtype=jnp.int32)
    alive_mask = (position < patch_count[0]).astype(jnp.float32)
    type_onehot = (
        patch_pft[0][:, None] == jnp.arange(pft_scale.shape[0], dtype=jnp.int32)[None, :]
    ).astype(jnp.float32)
    scaled = values * jnp.dot(type_onehot, pft_scale, precision=HIGH)
    col_table = jnp.stack([col_wt[0], col_lu[0].astype(jnp.float32)], axis=1)
    col_table = jnp.concatenate([col_table, jnp.zeros((block, 2), jnp.float32)], axis=0)
    lu_table = jnp.stack([lu_wt[0], lu_grid[0].astype(jnp.float32)], axis=1)
    lu_table = jnp.concatenate([lu_table, jnp.zeros((block, 2), jnp.float32)], axis=0)
    within = jnp.arange(block, dtype=jnp.int32)

    def gather_block(carry, entries):
        num_acc, den_acc = carry
        cols_blk, alive_blk, pwt_blk, scaled_blk = entries
        col_start = cols_blk[0]
        col_vals = window_pick(col_table, col_start, cols_blk - col_start, block)
        land_blk = col_vals[:, 1].astype(jnp.int32)
        land_start = land_blk[0]
        lu_vals = window_pick(lu_table, land_start, land_blk - land_start, block)
        home_blk = lu_vals[:, 1].astype(jnp.int32)
        weight_blk = alive_blk * pwt_blk * col_vals[:, 0] * lu_vals[:, 0]
        home_start = home_blk[0]
        cell_onehot = (within[:, None] == (home_blk - home_start)[None, :]).astype(jnp.float32)
        part_num = jnp.dot(cell_onehot, scaled_blk * weight_blk[:, None], precision=HIGH)
        part_den = jnp.dot(cell_onehot, weight_blk, precision=HIGH)
        old_num = lax.dynamic_slice_in_dim(num_acc, home_start, block, 0)
        old_den = lax.dynamic_slice_in_dim(den_acc, home_start, block, 0)
        num_acc = lax.dynamic_update_slice_in_dim(num_acc, old_num + part_num, home_start, 0)
        den_acc = lax.dynamic_update_slice_in_dim(den_acc, old_den + part_den, home_start, 0)
        return ((num_acc, den_acc), home_blk)

    start_acc = (
        jnp.zeros((cell_count + block, width_vars), jnp.float32),
        jnp.zeros((cell_count + block,), jnp.float32),
    )
    block_inputs = (
        patch_col[0].reshape(blocks, block),
        alive_mask.reshape(blocks, block),
        patch_wt[0].reshape(blocks, block),
        scaled.reshape(blocks, block, width_vars),
    )
    (num_acc, den_acc), home_blocks = lax.scan(gather_block, start_acc, block_inputs)
    cell_num = num_acc[:cell_count]
    cell_den = den_acc[:cell_count]
    target = cell_target[0]
    owner_dev = target // cell_count
    local_slot = target - owner_dev * cell_count
    same_owner = (owner_dev[:, None] == owner_dev[None, :]).astype(jnp.int32)
    earlier = (
        jnp.arange(cell_count, dtype=jnp.int32)[None, :]
        < jnp.arange(cell_count, dtype=jnp.int32)[:, None]
    ).astype(jnp.int32)
    rank_within = jnp.sum(same_owner * earlier, axis=1)
    slot = owner_dev * capacity + rank_within
    slot_onehot = (jnp.arange(slot_total, dtype=jnp.int32)[:, None] == slot[None, :]).astype(
        jnp.float32
    )
    slot_used = jnp.sum(slot_onehot, axis=1)
    send_slot = jnp.dot(slot_onehot, local_slot.astype(jnp.float32), precision=HIGH) + (
        1.0 - slot_used
    ) * float(cell_count)
    send_slot = send_slot.reshape(n_clump, n_group, capacity)
    cell_mean = cell_num / jnp.maximum(cell_den, 1.0)[:, None]
    send_mean = jnp.dot(slot_onehot, cell_mean, precision=HIGH)
    outgoing = (send_mean.reshape(n_clump, n_group, capacity, width_vars), send_slot)
    incoming = (
        exchange_both(outgoing[0], ("clump", "grp"), ("clump", "grp"), (0, 1), (0, 1)),
        exchange_both(outgoing[1], ("clump", "grp"), ("clump", "grp"), (0, 1), (0, 1)),
    )
    slot_ids = incoming[-1].reshape(-1).astype(jnp.int32)
    owner_onehot = (slot_ids[:, None] == jnp.arange(cell_count, dtype=jnp.int32)[None, :]).astype(
        jnp.float32
    )
    owned_mean = jnp.dot(owner_onehot.T, incoming[0].reshape(-1, width_vars), precision=HIGH)
    grid_merged = cpl_frac[:, None] * owned_mean + (1.0 - cpl_frac)[:, None] * cpl_field
    reply_rows = jnp.dot(owner_onehot, grid_merged, precision=HIGH).reshape(
        n_clump, n_group, capacity, width_vars
    )
    returned = exchange_both(reply_rows, ("clump", "grp"), ("clump", "grp"), (0, 1), (0, 1))
    cell_merged = jnp.dot(slot_onehot.T, returned.reshape(slot_total, width_vars), precision=HIGH)
    merged_table = jnp.concatenate(
        [cell_merged, jnp.zeros((block, width_vars), jnp.float32)], axis=0
    )

    def spread_block(entries):
        home_blk, alive_blk, scaled_blk = entries
        home_start = home_blk[0]
        picked = window_pick(merged_table, home_start, home_blk - home_start, block)
        return alive_blk[:, None] * (scaled_blk - picked)

    anomaly = lax.map(
        spread_block,
        (home_blocks, alive_mask.reshape(blocks, block), scaled.reshape(blocks, block, width_vars)),
    )
    return (grid_merged, anomaly.reshape(1, patches, width_vars))


def solution(mesh):
    return jax.shard_map(
        per_device,
        mesh=mesh,
        in_specs=(
            P(("clump", "grp"), None, None),
            P(("clump", "grp"), None),
            P(("clump", "grp"), None),
            P(("clump", "grp"), None),
            P(("clump", "grp"), None),
            P(("clump", "grp"), None),
            P(("clump", "grp"), None),
            P(("clump", "grp"), None),
            P(("clump", "grp"), None),
            P(("clump", "grp")),
            P(),
            P(("clump", "grp")),
            P(("clump", "grp"), None),
        ),
        out_specs=(P(("clump", "grp"), None), P(("clump", "grp"), None, None)),
        check_vma=False,
    )
```

profile of v0, /device:TPU:1, one launch (start us, length us, event | category | flops | bytes accessed | tf_op | source)
XLA Modules:
  0.0 160.4 jit_solution(8145341987746547489)
XLA Ops:
  0.7 0.7 and_select_fusion
  2.1 0.9 reshape_transpose_transpose_reshape_reshape_reshape.9
  3.0 24.3 %all-to-all-start = ((f32[512,1,1,2]{3,2,1,0:T(1,128)}), f32[512,1,1,2]{3,2,1,0:T(1,128)S(1)}, u32[]{:S(2)}, u32[]{:S(2)}) async-start(f32[512,1,1,2]{3,2,1,0:T(1,128)} %bitcast.11), calls=%async_computation | async-start | bytes 524288 | tf_op jit(solution)/shard_map/all_to_all | solution.py:27
  28.8 0.7 copy-done.7
  30.2 0.7 reduce.6
  31.5 0.7 reduce.7
  32.2 0.7 copy-done.9
  32.9 0.7 copy-done.8
  33.6 0.7 copy-done.10
  34.3 26.8 %while.26 = (s32[]{:T(128)}, f32[640,64]{0,1:T(8,128)S(1)}, f32[640]{0:T(1024)S(1)}, s32[2,512]{1,0:T(2,128)S(1)}, s32[2,512]{1,0:T(2,128)S(1)}, /*index=5*/f32[...) while((s32[]{:T(128)}, f32[640,64]{0,1:T(8,128)S(1)}, ...), condition=%wide.region_3.4_spmd.clone, body=%wide.region_2.3_spmd.clone.sunk | while | flops 218176016 | bytes 1268031 | solution.py:106
  36.8 0.7 dynamic-slice_subtract_fusion.5
  45.2 0.7 convolution_add_fusion.2
  46.0 0.8 dynamic_update_slice.24
  50.0 0.7 dynamic-slice_subtract_fusion.5
  58.5 0.7 convolution_add_fusion.2
  59.3 1.0 dynamic_update_slice.24
  61.4 1.3 reshape.185
  62.7 21.6 %all-to-all-start.1 = ((f32[512,1,128]{2,1,0:T(1,128)}), f32[512,1,128]{2,1,0:T(1,128)S(1)}, u32[]{:S(2)}, u32[]{:S(2)}) async-start(f32[512,1,128]{2,1,0:T(1,128)} %reshape.185), calls=%async_computation.1 | async-start | bytes 524288 | tf_op jit(solution)/shard_map/all_to_all | solution.py:27
  84.8 24.5 %all-to-all-done.1 = f32[512,1,128]{2,1,0:T(1,128)S(1)} async-done(((f32[512,1,128]{2,1,0:T(1,128)}), f32[512,1,128]{2,1,0:T(1,128)S(1)}, u32[]{:S(2)}, u32[]{:S(2)}) %all-to-all-start.1) | async-done | bytes 262176 | tf_op jit(solution)/shard_map/all_to_all | solution.py:27
  109.8 1.2 reduce.8
  111.7 0.7 fusion.21
  113.1 1.3 reshape.187
  114.3 8.3 %all-to-all-start.2 = ((f32[512,1,128]{2,1,0:T(1,128)}), f32[512,1,128]{2,1,0:T(1,128)S(1)}, u32[]{:S(2)}, u32[]{:S(2)}) async-start(f32[512,1,128]{2,1,0:T(1,128)} %reshape.187), calls=%async_computation.2 | async-start | bytes 524288 | tf_op jit(solution)/shard_map/all_to_all | solution.py:27
  122.7 23.9 %all-to-all-done.2 = f32[512,1,128]{2,1,0:T(1,128)S(1)} async-done(((f32[512,1,128]{2,1,0:T(1,128)}), f32[512,1,128]{2,1,0:T(1,128)S(1)}, u32[]{:S(2)}, u32[]{:S(2)}) %all-to-all-start.2) | async-done | bytes 262176 | tf_op jit(solution)/shard_map/all_to_all | solution.py:27
  146.6 1.2 reduce.9
  148.7 10.7 %while.25 = (s32[]{:T(128)}, f32[2,512,64]{1,0,2:T(2,128)S(1)}, f32[2,512]{1,0:T(2,128)S(1)}, f32[2,512,64]{1,0,2:T(2,128)S(1)}, s32[2,512]{1,0:T(2,128)S(1)}, /...) while((s32[]{:T(128)}, f32[2,512,64]{1,0,2:T(2,128)S(1)}, f32[2,512]{1,0:T(2,128)S(1)}, ...), condition=%wide.region_5.6_spmd, body=%wide.region_4.5_spmd.sunk | while | flops 201654784 | bytes 1192099 | solution.py:155
  151.2 0.7 dynamic-slice_subtract_fusion.4
  152.0 0.7 fusion.58
  152.9 1.2 dynamic_update_slice.22
  157.3 0.7 fusion.58
  158.2 1.2 dynamic_update_slice.22
  159.4 0.9 reshape.161
  (94 shorter events, 19.1 us)
Async XLA Ops:
  0.6 26.7 %copy-start = (f32[16,64]{1,0:T(8,128)S(1)}, f32[16,64]{1,0:T(8,128)}, u32[]{:S(2)}) copy-start(f32[16,64]{1,0:T(8,128)} %param.27) | copy-start | bytes 12292
  0.6 0.7 copy-start.12
  3.0 24.3 %copy-start.1 = (f32[1,1024,64]{1,2,0:T(8,128)S(1)}, f32[1,1024,64]{1,2,0:T(8,128)}, u32[]{:S(2)}) copy-start(f32[1,1024,64]{1,2,0:T(8,128)} %param.17) | copy-start | bytes 786436
  3.0 24.3 %copy-start.4 = (s32[1,1024]{1,0:T(1,128)S(1)}, s32[1,1024]{1,0:T(1,128)}, u32[]{:S(2)}) copy-start(s32[1,1024]{1,0:T(1,128)} %param.18) | copy-start | bytes 12292
  3.0 59.7 %all-to-all-start = ((f32[512,1,1,2]{3,2,1,0:T(1,128)}), f32[512,1,1,2]{3,2,1,0:T(1,128)S(1)}, u32[]{:S(2)}, u32[]{:S(2)}) async-start(f32[512,1,1,2]{3,2,1,0:T(1,128)} %bitcast.11), calls=%async_computation | async-start | bytes 524288 | tf_op jit(solution)/shard_map/all_to_all | solution.py:27
  28.8 0.7 copy-start.7
  29.5 0.7 copy-start.5
  30.8 0.7 copy-start.6
  32.2 0.7 copy-start.9
  32.9 0.7 copy-start.8
  33.6 0.7 copy-start.10
  62.7 21.6 %copy-start.11 = (f32[128]{0:T(128)S(1)}, f32[128]{0:T(128)}, u32[]{:S(2)}) copy-start(f32[128]{0:T(128)} %param.28) | copy-start | bytes 1540
  62.7 46.6 %all-to-all-start.1 = ((f32[512,1,128]{2,1,0:T(1,128)}), f32[512,1,128]{2,1,0:T(1,128)S(1)}, u32[]{:S(2)}, u32[]{:S(2)}) async-start(f32[512,1,128]{2,1,0:T(1,128)} %reshape.185), calls=%async_computation.1 | async-start | bytes 524288 | tf_op jit(solution)/shard_map/all_to_all | solution.py:27
  111.0 0.8 copy-start.3
  112.5 0.6 copy-start.2
  114.3 32.3 %all-to-all-start.2 = ((f32[512,1,128]{2,1,0:T(1,128)}), f32[512,1,128]{2,1,0:T(1,128)S(1)}, u32[]{:S(2)}, u32[]{:S(2)}) async-start(f32[512,1,128]{2,1,0:T(1,128)} %reshape.187), calls=%async_computation.2 | async-start | bytes 524288 | tf_op jit(solution)/shard_map/all_to_all | solution.py:27
where the time goes:
time: 161 us; the launch traced here: 160 us
  starting transfers between devices  54.3 us (34%)
  waiting for transfers between devices  48.4 us (30%)
  local copies, waits for them, and re-layouts  20 us (12%)
  loops' own time  15.8 us (10%)
  other arithmetic  10.6 us (7%)
  matrix products  9.64 us (6%)
    all_to_all x3, starting transfers between devices, exchange_both(): parts = lax.all_to_all(parts, axis, split_axis=0, concat_axis=0, tiled=True)  54.3 us
    all_to_all x3, waiting for transfers between devices, exchange_both(): parts = lax.all_to_all(parts, axis, split_axis=0, concat_axis=0, tiled=True)  48.4 us
    another operation x1, loops' own time, per_device(): lax.scan(gather_block, start_acc, block_inputs)  11.8 us
    unnamed x32, local copies, waits for them, and re-layouts  7.79 us
    another operation x1, loops' own time, per_device(): lax.map(spread_block, (home_blocks, alive_mask.reshape(blocks, block), sc...  3.99 us
    dot_general x6, matrix products, window_pick(): return jnp.dot(onehot, window, precision=HIGH)  3.97 us
  transfers between devices with their start and end apart: 3, of which 2 were waited for; matrix products, arithmetic and copies ran while one was open for 13% of the time, Pallas kernels for 0%

commit v1 on v0

v1 whole, which is shorter than its diff:
```python
import jax
import jax.numpy as jnp
from jax import lax
from jax.experimental import pallas as pl
from jax.experimental.pallas import tpu as pltpu
from jax.sharding import PartitionSpec as P

F32 = jnp.float32
BF16 = jnp.bfloat16
AXES = ("clump", "grp")


def pieces(x, count):
    parts = []
    for _ in range(count):
        part = x.astype(BF16)
        parts.append(part)
        x = x - part.astype(F32)
    return parts


def contract(a, b, da, db):
    return lax.dot_general(a, b, (((da,), (db,)), ((), ())), preferred_element_type=F32)


def onehot(mask):
    return jnp.where(mask, F32(1.0), F32(0.0)).astype(BF16)


def iota(shape, dim):
    return lax.broadcasted_iota(jnp.int32, shape, dim)


def pair_masks(target, cells, devices):
    owner = target // cells
    owner_rows = jnp.broadcast_to(owner, (cells, cells)).astype(F32)
    same = owner_rows.T == owner_rows
    earlier = iota((cells, cells), 0) < iota((cells, cells), 1)
    rank = jnp.max(jnp.where(same & earlier, F32(1.0), F32(0.0)), axis=0, keepdims=True)
    hit = iota((devices, cells), 0) == owner
    return onehot(hit & (rank < 0.5)), onehot(hit & (rank > 0.5))


def side_by_side(x):
    hi, lo = pieces(x, 2)
    both = jnp.concatenate([hi, lo], axis=1)
    zero = jnp.zeros_like(both)
    return jnp.concatenate(
        [jnp.concatenate([both, zero], axis=1), jnp.concatenate([zero, both], axis=1)], axis=0
    )


def from_rows(rows, first, second):
    width = rows.shape[1] // 2
    hi, lo = pieces(rows, 2)
    one = contract(hi, first, 0, 0) + contract(lo, first, 0, 0)
    two = contract(hi, second, 0, 0) + contract(lo, second, 0, 0)
    return one[:width] + two[width:]


def gather_kernel(
    count_ref,
    flux_ref,
    pft_ref,
    wt_ref,
    col_ref,
    col_wt_ref,
    col_lu_ref,
    lu_wt_ref,
    lu_grid_ref,
    target_ref,
    scale_ref,
    send_ref,
    scaled_ref,
    home_ref,
):
    width, patches = flux_ref.shape
    cells = target_ref.shape[1]
    devices = send_ref.shape[0] // 2
    columns = col_wt_ref.shape[1]
    units = lu_wt_ref.shape[1]
    types = scale_ref.shape[0]

    unit_table = jnp.concatenate(
        pieces(lu_wt_ref[...], 3)
        + [lu_grid_ref[...].astype(F32).astype(BF16), jnp.zeros((12, units), BF16)],
        axis=0,
    )
    unit_of = onehot(iota((units, columns), 0) == col_lu_ref[...])
    picked = contract(unit_table, unit_of, 1, 0)
    col_weight = col_wt_ref[...] * (picked[0:1] + picked[1:2] + picked[2:3])
    col_table = jnp.concatenate(
        pieces(col_weight, 3) + [picked[3:4].astype(BF16), jnp.zeros((12, columns), BF16)], axis=0
    )
    col_of = onehot(iota((columns, patches), 0) == col_ref[...])
    picked = contract(col_table, col_of, 1, 0)
    alive = iota((1, patches), 1) < count_ref[0]
    weight = jnp.where(
        alive, wt_ref[...] * (picked[0:1] + picked[1:2] + picked[2:3]), F32(0.0)
    )
    home = picked[3:4].astype(jnp.int32)
    home_ref[...] = home

    type_of = onehot(iota((types, patches), 0) == pft_ref[...])
    scale_parts = jnp.concatenate(pieces(scale_ref[...], 3), axis=0)
    factor = contract(scale_parts, jnp.concatenate([type_of] * 3, axis=0), 0, 0)
    scaled = flux_ref[...] * factor
    scaled_ref[...] = scaled

    cell_of = onehot(iota((cells, patches), 0) == home)
    terms = jnp.concatenate([scaled * weight, weight, jnp.zeros((15, patches), F32)], axis=0)
    sums = [contract(part, cell_of, 1, 1) for part in pieces(terms, 2)]
    total = sums[0] + sums[1]
    mean = total[:width] / jnp.maximum(total[width : width + 1], 1.0)

    first, second = pair_masks(target_ref[...], cells, devices)
    masks = jnp.concatenate([first, first, second, second], axis=1)
    send_ref[pl.ds(0, devices, 2), :] = contract(masks, side_by_side(mean), 1, 1)
    slot = (target_ref[...] % cells + 1).astype(F32).astype(BF16)
    pad = jnp.zeros((1, cells), BF16)
    slot_rows = jnp.concatenate(
        [
            jnp.concatenate([slot, pad, pad, pad], axis=1),
            jnp.concatenate([pad, pad, slot, pad], axis=1),
            jnp.zeros((2 * width - 2, 4 * cells), BF16),
        ],
        axis=0,
    )
    send_ref[pl.ds(1, devices, 2), :] = contract(masks, slot_rows, 1, 1)


def merge_kernel(got_ref, frac_ref, field_ref, merged_ref, reply_ref):
    width, cells = field_ref.shape
    devices = reply_ref.shape[0]
    rows = got_ref[pl.ds(0, devices, 2), :]
    slots = got_ref[pl.ds(1, devices, 2), :].astype(jnp.int32) - 1
    lane = iota((devices, cells), 1)
    first = onehot(lane == slots[:, 0:1])
    second = onehot(lane == slots[:, 1:2])
    frac = frac_ref[...]
    merged = frac * from_rows(rows, first, second) + (1.0 - frac) * field_ref[...]
    merged_ref[...] = merged
    masks = jnp.concatenate([first, first, second, second], axis=1)
    reply_ref[...] = contract(masks, side_by_side(merged), 1, 1)


def spread_kernel(count_ref, back_ref, target_ref, home_ref, scaled_ref, out_ref):
    width, patches = scaled_ref.shape
    cells = target_ref.shape[1]
    devices = back_ref.shape[0]
    first, second = pair_masks(target_ref[...], cells, devices)
    merged = from_rows(back_ref[...], first, second)
    cell_of = onehot(iota((cells, patches), 0) == home_ref[...])
    parts = contract(jnp.concatenate(pieces(merged, 2), axis=0), cell_of, 1, 0)
    picked = parts[:width] + parts[width:]
    alive = iota((1, patches), 1) < count_ref[0]
    out_ref[...] = jnp.where(alive, scaled_ref[...] - picked, F32(0.0))


VMEM = pl.BlockSpec(memory_space=pltpu.VMEM)
SMEM = pl.BlockSpec(memory_space=pltpu.SMEM)


def exchange(x):
    return lax.all_to_all(x, AXES, split_axis=0, concat_axis=0, tiled=True)


def per_device(
    flux,
    patch_pft,
    patch_wt,
    patch_col,
    col_wt,
    col_lu,
    lu_wt,
    lu_grid,
    cell_target,
    patch_count,
    pft_scale,
    cpl_frac,
    cpl_field,
):
    devices = lax.axis_size("clump") * lax.axis_size("grp")
    patches, width = flux.shape[1:]
    cells = cell_target.shape[1]
    shape = jax.ShapeDtypeStruct
    send, scaled, home = pl.pallas_call(
        gather_kernel,
        out_shape=(
            shape((2 * devices, 2 * width), F32),
            shape((width, patches), F32),
            shape((1, patches), jnp.int32),
        ),
        in_specs=[SMEM] + [VMEM] * 10,
        out_specs=(VMEM, VMEM, VMEM),
        name="gather_cells",
    )(
        patch_count,
        flux[0].T,
        patch_pft,
        patch_wt,
        patch_col,
        col_wt,
        col_lu,
        lu_wt,
        lu_grid,
        cell_target,
        pft_scale,
    )
    got = exchange(send.reshape(devices, 2, 2 * width)).reshape(2 * devices, 2 * width)
    merged, reply = pl.pallas_call(
        merge_kernel,
        out_shape=(shape((width, cells), F32), shape((devices, 2 * width), F32)),
        in_specs=[VMEM] * 3,
        out_specs=(VMEM, VMEM),
        name="merge_cells",
    )(got, cpl_frac.reshape(1, cells), cpl_field.T)
    back = exchange(reply.reshape(devices, 1, 2 * width)).reshape(devices, 2 * width)
    anomaly = pl.pallas_call(
        spread_kernel,
        out_shape=shape((width, patches), F32),
        in_specs=[SMEM] + [VMEM] * 4,
        out_specs=VMEM,
        name="spread_cells",
    )(patch_count, back, cell_target, home, scaled)
    return merged.T, anomaly.T[None]


def solution(mesh):
    rows = P(AXES, None)
    return jax.shard_map(
        per_device,
        mesh=mesh,
        in_specs=(
            P(AXES, None, None),
            rows,
            rows,
            rows,
            rows,
            rows,
            rows,
            rows,
            rows,
            P(AXES),
            P(),
            P(AXES),
            rows,
        ),
        out_specs=(rows, P(AXES, None, None)),
        check_vma=False,
    )
```

time: 161 us -> 104 us (0.65)
  blocking collectives: 0 us -> 94.6 us
  starting transfers between devices: 54.3 us -> 0 us
  waiting for transfers between devices: 48.4 us -> 0 us
  local copies, waits for them, and re-layouts: 20 us -> 0 us
  loops' own time: 15.8 us -> 0 us
  other arithmetic: 10.6 us -> 0 us
  matrix products: 9.64 us -> 0 us
  Pallas kernels: 0 us -> 8.06 us
    all_to_all x0 -> x2, blocking collectives: none -> 94.6 us  [exchange(): return lax.all_to_all(x, AXES, split_axis=0, concat_axis=0, tiled=True)]
    all_to_all x3 -> x0, starting transfers between devices: 54.3 us -> none  [exchange_both(): parts = lax.all_to_all(parts, axis, split_axis=0, concat_axis=0, tiled=True)]
    all_to_all x3 -> x0, waiting for transfers between devices: 48.4 us -> none  [exchange_both(): parts = lax.all_to_all(parts, axis, split_axis=0, concat_axis=0, tiled=True)]
    another operation x2 -> x0, loops' own time: 15.8 us -> none  [the longest x1 11.8 us: per_device(): lax.scan(gather_block, start_acc, block_inputs)]
    dot_general x16 -> x0, matrix products: 9.64 us -> none  [the longest x6 3.97 us: window_pick(): return jnp.dot(onehot, window, precision=HIGH)]
    pallas_call x0 -> x3, Pallas kernels: none -> 8.06 us  [the longest x1 3.18 us: per_device(): pl.pallas_call(gather_kernel, out_shape=(shape((2 * devices, 2 * width),...]
    unnamed x32 -> x0, local copies, waits for them, and re-layouts: 7.79 us -> none
    sub x9 -> x0, other arithmetic: 5.22 us -> none  [the longest x2 1.31 us: gather_block(): col_vals = window_pick(col_table, col_start, cols_blk - col_start, block)]
  transfers between devices with their start and end apart: 3 -> 0, of which waited for: 2 -> 0; matrix products, arithmetic and copies ran while one was open for 13% -> 0% of each run, Pallas kernels for 0% -> 0%
where the time goes in v1:
time: 104 us
  blocking collectives  94.6 us (91%)
  Pallas kernels  8.06 us (8%)
  between operations  1.28 us (1%)
    all_to_all x2, blocking collectives, exchange(): return lax.all_to_all(x, AXES, split_axis=0, concat_axis=0, tiled=True)  94.6 us
    pallas_call x1, Pallas kernels, per_device(): pl.pallas_call(gather_kernel, out_shape=(shape((2 * devices, 2 * width),...  3.18 us
    pallas_call x1, Pallas kernels, per_device(): pl.pallas_call(merge_kernel, out_shape=(shape((width, cells), F32), shape...  2.52 us
    pallas_call x1, Pallas kernels, per_device(): pl.pallas_call(spread_kernel, out_shape=shape((width, patches), F32), in_...  2.37 us

profile of v1, /device:TPU:1, one launch (start us, length us, event | category | flops | bytes accessed | tf_op | source)
XLA Modules:
  0.0 103.9 jit_solution(9566270827405366268)
XLA Ops:
  1.3 3.2 %gather_cells.1 = (f32[1024,128]{1,0:T(8,128)}, f32[64,1024]{1,0:T(8,128)}, s32[1,1024]{1,0:T(1,128)}) custom-call(s32[1]{0:T(128)S(6)} %copy.16.count_ref, f32[64,1024]{1,0:T(8,128)} %bitcast.18, s32[1,1024]{1,0:T(1,128)} %pft_ref.1, f32[1,1024]{1,0:T(1,128)} %wt_ref.1, s32[1,1024]{1,0:T(1,128)} %col_ref.1, f32[1,512]{1,0:T(1,128)} %col_wt_ref.1, ...), custom_call_target="tpu_custom_call" | custom-call | tf_op jit(solution)/shard_map/gather_cells/pallas_call | solution.py:187
  4.5 60.6 %all_to_all.10 = f32[512,2,128]{2,1,0:T(2,128)} all-to-all(f32[512,2,128]{2,1,0:T(2,128)} %bitcast.17), channel_id=1, replica_groups=mesh['clump'=128,'grp'=4] {'clump','grp'}, dimensions={0} | all-to-all | bytes 1048576 | tf_op jit(solution)/shard_map/all_to_all | solution.py:165
  65.1 2.5 %merge_cells.1 = (f32[64,128]{1,0:T(8,128)}, f32[512,128]{1,0:T(8,128)}) custom-call(f32[1024,128]{1,0:T(8,128)} %bitcast.15, f32[1,128]{1,0:T(1,128)} %bitcast.22, f32[64,128]{1,0:T(8,128)} %bitcast.21), custom_call_target="tpu_custom_call" | custom-call | tf_op jit(solution)/shard_map/merge_cells/pallas_call | solution.py:211
  67.6 34.0 %all_to_all.11 = f32[512,1,128]{2,1,0:T(1,128)} all-to-all(f32[512,1,128]{2,1,0:T(1,128)} %bitcast.20), channel_id=1, replica_groups=mesh['clump'=128,'grp'=4] {'clump','grp'}, dimensions={0} | all-to-all | bytes 524288 | tf_op jit(solution)/shard_map/all_to_all | solution.py:165
  101.6 2.4 %spread_cells.1 = f32[64,1024]{1,0:T(8,128)} custom-call(s32[1]{0:T(128)S(6)} %copy.16.count_ref, f32[512,128]{1,0:T(8,128)} %bitcast.16, s32[1,128]{1,0:T(1,128)} %target_ref.3, s32[1,1024]{1,0:T(1,128)} %get-tuple-element.10.home_ref, f32[64,1024]{1,0:T(8,128)} %get-tuple-element.11.scaled_ref), custom_call_target="tpu_custom_call" | custom-call | tf_op jit(solution)/shard_map/spread_cells/pallas_call | solution.py:219

commit v2 on v1

v2 whole, which is shorter than its diff:
```python
import jax
import jax.numpy as jnp
from jax import lax
from jax.experimental import pallas as pl
from jax.experimental.pallas import tpu as pltpu
from jax.sharding import PartitionSpec as P

F32 = jnp.float32
BF16 = jnp.bfloat16
AXES = ("clump", "grp")
PLANES = 16


def pieces(x, count):
    parts = []
    for _ in range(count):
        part = x.astype(BF16)
        parts.append(part)
        x = x - part.astype(F32)
    return parts


def contract(a, b, da, db):
    return lax.dot_general(a, b, (((da,), (db,)), ((), ())), preferred_element_type=F32)


def onehot(mask):
    return jnp.where(mask, F32(1.0), F32(0.0)).astype(BF16)


def iota(shape, dim):
    return lax.broadcasted_iota(jnp.int32, shape, dim)


def earlier_mate(owner, cells):
    owner_rows = jnp.broadcast_to(owner, (cells, cells)).astype(F32)
    same = owner_rows.T == owner_rows
    earlier = iota((cells, cells), 0) < iota((cells, cells), 1)
    return jnp.max(jnp.where(same & earlier, F32(1.0), F32(0.0)), axis=0, keepdims=True)


def pair_masks(target, cells, devices):
    owner = target // cells
    rank = earlier_mate(owner, cells)
    hit = iota((devices, cells), 0) == owner
    return onehot(hit & (rank < 0.5)), onehot(hit & (rank > 0.5))


def side_by_side(x):
    hi, lo = pieces(x, 2)
    both = jnp.concatenate([hi, lo], axis=1)
    zero = jnp.zeros_like(both)
    return jnp.concatenate(
        [jnp.concatenate([both, zero], axis=1), jnp.concatenate([zero, both], axis=1)], axis=0
    )


def from_rows(rows, first, second):
    width = rows.shape[1] // 2
    hi, lo = pieces(rows, 2)
    one = contract(hi, first, 0, 0) + contract(lo, first, 0, 0)
    two = contract(hi, second, 0, 0) + contract(lo, second, 0, 0)
    return one[:width] + two[width:]


def gather_kernel(
    count_ref,
    flux_ref,
    pft_ref,
    wt_ref,
    col_ref,
    col_wt_ref,
    col_lu_ref,
    lu_wt_ref,
    lu_grid_ref,
    target_ref,
    scale_ref,
    send_ref,
    scaled_ref,
    cell_of_ref,
    first_ref,
    second_ref,
    *scratch,
):
    held, sems = scratch[:-1], scratch[-1]
    given = (
        col_lu_ref,
        lu_wt_ref,
        lu_grid_ref,
        col_wt_ref,
        col_ref,
        pft_ref,
        scale_ref,
        wt_ref,
        target_ref,
        flux_ref,
    )
    copies = [
        pltpu.make_async_copy(src, dst, sems.at[i]) for i, (src, dst) in enumerate(zip(given, held))
    ]
    for copy in copies:
        copy.start()
    (
        col_lu_ref,
        lu_wt_ref,
        lu_grid_ref,
        col_wt_ref,
        col_ref,
        pft_ref,
        scale_ref,
        wt_ref,
        target_ref,
        flux_ref,
    ) = held
    for copy in copies[:4]:
        copy.wait()
    width, patches = flux_ref.shape
    cells = target_ref.shape[1]
    devices = send_ref.shape[0] - PLANES
    columns = col_wt_ref.shape[1]
    units = lu_wt_ref.shape[1]
    types = scale_ref.shape[0]

    unit_table = jnp.concatenate(
        pieces(lu_wt_ref[...], 3)
        + [lu_grid_ref[...].astype(F32).astype(BF16), jnp.zeros((12, units), BF16)],
        axis=0,
    )
    unit_of = onehot(iota((units, columns), 0) == col_lu_ref[...])
    picked = contract(unit_table, unit_of, 1, 0)
    col_weight = col_wt_ref[...] * (picked[0:1] + picked[1:2] + picked[2:3])
    col_table = jnp.concatenate(
        pieces(col_weight, 3) + [picked[3:4].astype(BF16), jnp.zeros((12, columns), BF16)], axis=0
    )
    copies[4].wait()
    col_of = onehot(iota((columns, patches), 0) == col_ref[...])
    picked = contract(col_table, col_of, 1, 0)
    alive = iota((1, patches), 1) < count_ref[0]
    copies[7].wait()
    weight = jnp.where(
        alive, wt_ref[...] * (picked[0:1] + picked[1:2] + picked[2:3]), F32(0.0)
    )
    home = picked[3:4].astype(jnp.int32)

    copies[5].wait()
    copies[6].wait()
    type_of = onehot(iota((types, patches), 0) == pft_ref[...])
    scale_parts = jnp.concatenate(pieces(scale_ref[...], 3), axis=0)
    factor = contract(scale_parts, jnp.concatenate([type_of] * 3, axis=0), 0, 0)
    copies[9].wait()
    scaled = flux_ref[...] * factor
    scaled_ref[...] = scaled

    cell_of = onehot(iota((cells, patches), 0) == home)
    cell_of_ref[...] = cell_of
    terms = jnp.concatenate([scaled * weight, weight, jnp.zeros((15, patches), F32)], axis=0)
    sums = [contract(part, cell_of, 1, 1) for part in pieces(terms, 2)]
    total = sums[0] + sums[1]
    mean = total[:width] / jnp.maximum(total[width : width + 1], 1.0)

    copies[8].wait()
    first, second = pair_masks(target_ref[...], cells, devices)
    first_ref[...] = first
    second_ref[...] = second
    masks = jnp.concatenate([first, first, second, second], axis=1)
    rows = contract(masks, side_by_side(mean), 1, 1)
    plane = devices // PLANES
    target = target_ref[...]
    slot = (target % cells + 1).astype(F32)
    owner = target // cells
    rank = earlier_mate(owner, cells)
    lane = owner % plane + jnp.where(rank > 0.5, plane, 0)
    left = jnp.where(iota((PLANES, cells), 0) == owner // plane, slot, F32(0.0)).astype(BF16)
    right = onehot(iota((2 * width, cells), 0) == lane)
    slots = contract(left, right, 1, 1)
    for z in range(PLANES):
        send_ref[pl.ds(z * (plane + 1), plane), :] = rows[z * plane : (z + 1) * plane]
    send_ref[pl.ds(plane, PLANES, plane + 1), :] = slots


def turn_kernel(got_ref, send_ref):
    place = got_ref.shape[0] // PLANES - 1
    for z in range(PLANES):
        rows = got_ref[pl.ds(z * (place + 1), place), :]
        send_ref[pl.ds(z, place, PLANES + 1), :] = rows
    slots = got_ref[pl.ds(place, PLANES, place + 1), :]
    lanes = slots.shape[1]
    turned = jnp.concatenate([slots, jnp.zeros((lanes - PLANES, lanes), F32)], axis=0).T
    one, two = turned[:place], turned[place : 2 * place]
    send_ref[pl.ds(PLANES, place, PLANES + 1), :] = one + pltpu.roll(two, PLANES, 1)


def merge_kernel(got_ref, frac_ref, field_ref, merged_ref, reply_ref):
    width, cells = field_ref.shape
    devices = reply_ref.shape[0]
    place = devices // PLANES
    rows = jnp.concatenate(
        [got_ref[pl.ds(z, place, PLANES + 1), :] for z in range(PLANES)], axis=0
    )
    slots = got_ref[pl.ds(PLANES, place, PLANES + 1), :].astype(jnp.int32) - 1
    lane = iota((place, cells), 1)
    first, second = (
        jnp.concatenate(
            [onehot(lane == slots[:, k + z : k + z + 1]) for z in range(PLANES)], axis=0
        )
        for k in (0, PLANES)
    )
    frac = frac_ref[...]
    merged = frac * from_rows(rows, first, second) + (1.0 - frac) * field_ref[...]
    merged_ref[...] = merged
    masks = jnp.concatenate([first, first, second, second], axis=1)
    reply_ref[...] = contract(masks, side_by_side(merged), 1, 1)


def spread_kernel(count_ref, back_ref, first_ref, second_ref, cell_of_ref, scaled_ref, out_ref):
    width, patches = scaled_ref.shape
    merged = from_rows(back_ref[...], first_ref[...], second_ref[...])
    parts = contract(jnp.concatenate(pieces(merged, 2), axis=0), cell_of_ref[...], 1, 0)
    picked = parts[:width] + parts[width:]
    alive = iota((1, patches), 1) < count_ref[0]
    out_ref[...] = jnp.where(alive, scaled_ref[...] - picked, F32(0.0))


PARAMS = pltpu.CompilerParams(vmem_limit_bytes=12 << 20)
VMEM = pl.BlockSpec(memory_space=pltpu.VMEM)
HBM = pl.BlockSpec(memory_space=pltpu.HBM)
SMEM = pl.BlockSpec(memory_space=pltpu.SMEM)


def exchange(x, axis=AXES, groups=None):
    return lax.all_to_all(
        x, axis, split_axis=0, concat_axis=0, tiled=True, axis_index_groups=groups
    )


def per_device(
    flux,
    patch_pft,
    patch_wt,
    patch_col,
    col_wt,
    col_lu,
    lu_wt,
    lu_grid,
    cell_target,
    patch_count,
    pft_scale,
    cpl_frac,
    cpl_field,
):
    devices = lax.axis_size("clump") * lax.axis_size("grp")
    patches, width = flux.shape[1:]
    cells = cell_target.shape[1]
    shape = jax.ShapeDtypeStruct
    lanes = 2 * width
    place = devices // PLANES
    columns = lax.axis_size("clump") // PLANES
    along = [[z * columns + i for z in range(PLANES)] for i in range(columns)]
    across = [[z * place + i for i in range(place)] for z in range(PLANES)]
    send, scaled, cell_of, first, second = pl.pallas_call(
        gather_kernel,
        out_shape=(
            shape((devices + PLANES, lanes), F32),
            shape((width, patches), F32),
            shape((cells, patches), BF16),
            shape((devices, cells), BF16),
            shape((devices, cells), BF16),
        ),
        in_specs=[SMEM] + [HBM] * 10,
        out_specs=(VMEM,) * 5,
        scratch_shapes=[
            pltpu.VMEM(col_lu.shape, jnp.int32),
            pltpu.VMEM(lu_wt.shape, F32),
            pltpu.VMEM(lu_grid.shape, jnp.int32),
            pltpu.VMEM(col_wt.shape, F32),
            pltpu.VMEM(patch_col.shape, jnp.int32),
            pltpu.VMEM(patch_pft.shape, jnp.int32),
            pltpu.VMEM(pft_scale.shape, F32),
            pltpu.VMEM(patch_wt.shape, F32),
            pltpu.VMEM(cell_target.shape, jnp.int32),
            pltpu.VMEM((width, patches), F32),
            pltpu.SemaphoreType.DMA((10,)),
        ],
        compiler_params=PARAMS,
        name="gather_cells",
    )(
        patch_count,
        *(
            pltpu.with_memory_space_constraint(x, pltpu.HBM)
            for x in (
                flux[0].T,
                patch_pft,
                patch_wt,
                patch_col,
                col_wt,
                col_lu,
                lu_wt,
                lu_grid,
                cell_target,
                pft_scale,
            )
        ),
    )
    got = exchange(send.reshape(PLANES, 1, (place + 1) * lanes), "clump", along)
    send = pl.pallas_call(
        turn_kernel,
        out_shape=shape((place * (PLANES + 1), lanes), F32),
        in_specs=[VMEM],
        out_specs=VMEM,
        compiler_params=PARAMS,
        name="turn_rows",
    )(got.reshape(PLANES * (place + 1), lanes))
    got = exchange(send.reshape(place, 1, (PLANES + 1) * lanes), AXES, across)
    got = got.reshape(place * (PLANES + 1), lanes)
    merged, reply = pl.pallas_call(
        merge_kernel,
        out_shape=(shape((width, cells), F32), shape((devices, 2 * width), F32)),
        in_specs=[VMEM] * 3,
        out_specs=(VMEM, VMEM),
        compiler_params=PARAMS,
        name="merge_cells",
    )(got, cpl_frac.reshape(1, cells), cpl_field.T)
    back = exchange(reply.reshape(devices, 1, 2 * width)).reshape(devices, 2 * width)
    anomaly = pl.pallas_call(
        spread_kernel,
        out_shape=shape((width, patches), F32),
        in_specs=[SMEM] + [VMEM] * 5,
        out_specs=VMEM,
        compiler_params=PARAMS,
        name="spread_cells",
    )(patch_count, back, first, second, cell_of, scaled)
    return merged.T, anomaly.T[None]


def solution(mesh):
    rows = P(AXES, None)
    return jax.shard_map(
        per_device,
        mesh=mesh,
        in_specs=(
            P(AXES, None, None),
            rows,
            rows,
            rows,
            rows,
            rows,
            rows,
            rows,
            rows,
            P(AXES),
            P(),
            P(AXES),
            rows,
        ),
        out_specs=(rows, P(AXES, None, None)),
        check_vma=False,
    )
```

time: 104 us -> 93.8 us (0.902)
  blocking collectives: 94.6 us -> 86.5 us
  Pallas kernels: 8.06 us -> 5.01 us
    all_to_all x2 -> x3, blocking collectives: 94.6 us -> 86.5 us  [exchange(): lax.all_to_all(x, axis, split_axis=0, concat_axis=0, tiled=True, axis_ind...]
    pallas_call x1, Pallas kernels: 2.52 us -> 1.19 us  [per_device(): pl.pallas_call(merge_kernel, out_shape=(shape((width, cells), F32), shape...]
    pallas_call x1, Pallas kernels: 2.37 us -> 1.24 us  [per_device(): pl.pallas_call(spread_kernel, out_shape=shape((width, patches), F32), in_...]
    pallas_call x1 -> x2, Pallas kernels: 3.18 us -> 2.58 us  [the longest x1 2.47 us: per_device(): pl.pallas_call(gather_kernel, out_shape=(shape((devices + PLANES, lanes),...]
where the time goes in v2:
time: 93.8 us; the launch traced here: 93.5 us
  blocking collectives  86.5 us (92%)
  Pallas kernels  5.01 us (5%)
  between operations  1.29 us (1%)
    all_to_all x3, blocking collectives, exchange(): lax.all_to_all(x, axis, split_axis=0, concat_axis=0, tiled=True, axis_ind...  86.5 us
    pallas_call x1, Pallas kernels, per_device(): pl.pallas_call(gather_kernel, out_shape=(shape((devices + PLANES, lanes),...  2.47 us

profile of v2, /device:TPU:1, one launch (start us, length us, event | category | flops | bytes accessed | tf_op | source)
XLA Modules:
  0.0 93.5 jit_solution(6045862533298796747)
XLA Ops:
  1.3 2.5 %gather_cells.1 = (f32[528,128]{1,0:T(8,128)S(1)}, f32[64,1024]{1,0:T(8,128)S(1)}, bf16[128,1024]{1,0:T(8,128)(2,1)S(1)}, bf16[512,128]{1,0:T(8,128)(2,1)S(1)}, bf16[512,128]{1,0:T(8,128)(2,1)S(1)}) custom-call(s32[1]{0:T(128)S(6)} %copy.18.count_ref, f32[64,1024]{1,0:T(8,128)} %bitcast.26, s32[1,1024]{1,0:T(1,128)} %pft_ref.1, f32[1,1024]{1,0:T(1,128)} %wt_ref.1, ...), custom_call_target="tpu_custom_call" | custom-call | tf_op jit(solution)/shard_map/gather_cells/pallas_call | solution.py:260
  3.8 29.4 %all_to_all.15 = f32[16,1,4224]{2,1,0:T(1,128)S(1)} all-to-all(f32[16,1,4224]{2,1,0:T(1,128)S(1)} %bitcast.21), channel_id=1, replica_groups={{0,32,64,96,128,160,192,224,256,288,320,352,384,416,448,480},{4,36,68,1..., dimensions={0} | all-to-all | bytes 540672 | tf_op jit(solution)/shard_map/all_to_all | solution.py:231
  33.2 0.1 turn_rows.1
  33.3 0.0 copy-start
  33.3 21.9 %all_to_all.16 = f32[32,1,2176]{2,1,0:T(1,128)S(1)} all-to-all(f32[32,1,2176]{2,1,0:T(1,128)S(1)} %bitcast.18), channel_id=1, replica_groups={{0,1,2,3,4,5,6,7,8,9,10,11,12,13,14,15,16,17,18,19,20,21,22,23,24,25,26..., dimensions={0} | all-to-all | bytes 557056 | tf_op jit(solution)/shard_map/all_to_all | solution.py:231
  55.2 0.0 copy-start.1
  55.2 0.0 copy-done
  55.2 0.7 copy-done.1
  55.8 1.2 %merge_cells.1 = (f32[64,128]{1,0:T(8,128)}, f32[512,128]{1,0:T(8,128)S(1)}) custom-call(f32[544,128]{1,0:T(8,128)S(1)} %bitcast.17, f32[1,128]{1,0:T(1,128)S(1)} %bitcast.24, f32[64,128]{1,0:T(8,128)S(1)} %bitcast.23), custom_call_target="tpu_custom_call" | custom-call | tf_op jit(solution)/shard_map/merge_cells/pallas_call | solution.py:315
  57.0 35.2 %all_to_all.17 = f32[512,1,128]{2,1,0:T(1,128)S(1)} all-to-all(f32[512,1,128]{2,1,0:T(1,128)S(1)} %bitcast.22), channel_id=1, replica_groups=mesh['clump'=128,'grp'=4] {'clump','grp'}, dimensions={0} | all-to-all | bytes 524288 | tf_op jit(solution)/shard_map/all_to_all | solution.py:231
  92.3 1.2 %spread_cells.1 = f32[64,1024]{1,0:T(8,128)} custom-call(s32[1]{0:T(128)S(6)} %copy.18.count_ref, f32[512,128]{1,0:T(8,128)S(1)} %bitcast.20, bf16[512,128]{1,0:T(8,128)(2,1)S(1)} %get-tuple-element.12.first_ref, bf16[512,128]{1,0:T(8,128)(2,1)S(1)} %get-tuple-element.13.second_ref, bf16[128,1024]{1,0:T(8,128)(2,1)S(1)} %get-tuple-element.14.cell_of_ref, ...), custom_call_target="tpu_custom_call" | custom-call | tf_op jit(solution)/shard_map/spread_cells/pallas_call | solution.py:324
Async XLA Ops:
  33.3 21.9 %copy-start = (f32[128,64]{0,1:T(8,128)S(1)}, f32[128,64]{0,1:T(8,128)}, u32[]{:S(2)}) copy-start(f32[128,64]{0,1:T(8,128)} %param.25) | copy-start | bytes 98308
  55.2 0.7 copy-start.1

commit v3 on v2

--- a/solution.py
+++ b/solution.py
@@ -4,6 +4,7 @@
 from jax.experimental import pallas as pl
 from jax.experimental.pallas import tpu as pltpu
 from jax.sharding import PartitionSpec as P
+
 
 F32 = jnp.float32
 BF16 = jnp.bfloat16
@@ -42,7 +43,8 @@
 def pair_masks(target, cells, devices):
     owner = target // cells
     rank = earlier_mate(owner, cells)
-    hit = iota((devices, cells), 0) == owner
+    place = devices // PLANES
+    hit = iota((devices, cells), 0) == owner % place * PLANES + owner // place
     return onehot(hit & (rank < 0.5)), onehot(hit & (rank > 0.5))
 
 
@@ -75,7 +77,10 @@
     lu_grid_ref,
     target_ref,
     scale_ref,
+    field_ref,
+    frac_ref,
     send_ref,
+    table_ref,
     scaled_ref,
     cell_of_ref,
     first_ref,
@@ -98,7 +103,11 @@
     copies = [
         pltpu.make_async_copy(src, dst, sems.at[i]) for i, (src, dst) in enumerate(zip(given, held))
     ]
-    for copy in copies:
+    tables = [
+        pltpu.make_async_copy(field_ref, table_ref.at[pl.ds(0, field_ref.shape[0])], sems.at[10]),
+        pltpu.make_async_copy(frac_ref, table_ref.at[pl.ds(field_ref.shape[0], 1)], sems.at[11]),
+    ]
+    for copy in copies + tables:
         copy.start()
     (
         col_lu_ref,
@@ -116,7 +125,7 @@
         copy.wait()
     width, patches = flux_ref.shape
     cells = target_ref.shape[1]
-    devices = send_ref.shape[0] - PLANES
+    devices = send_ref.shape[0] // (PLANES + 1) * PLANES
     columns = col_wt_ref.shape[1]
     units = lu_wt_ref.shape[1]
     types = scale_ref.shape[0]
@@ -164,52 +173,70 @@
     second_ref[...] = second
     masks = jnp.concatenate([first, first, second, second], axis=1)
     rows = contract(masks, side_by_side(mean), 1, 1)
-    plane = devices // PLANES
+    place = devices // PLANES
     target = target_ref[...]
     slot = (target % cells + 1).astype(F32)
     owner = target // cells
     rank = earlier_mate(owner, cells)
-    lane = owner % plane + jnp.where(rank > 0.5, plane, 0)
-    left = jnp.where(iota((PLANES, cells), 0) == owner // plane, slot, F32(0.0)).astype(BF16)
+    lane = owner // place + jnp.where(rank > 0.5, PLANES, 0)
+    left = jnp.where(iota((place, cells), 0) == owner % place, slot, F32(0.0)).astype(BF16)
     right = onehot(iota((2 * width, cells), 0) == lane)
     slots = contract(left, right, 1, 1)
+    for i in range(place):
+        send_ref[pl.ds(i * (PLANES + 1), PLANES), :] = rows[i * PLANES : (i + 1) * PLANES]
+    send_ref[pl.ds(PLANES, place, PLANES + 1), :] = slots
+    for copy in tables:
+        copy.wait()
+
+
+def turn_kernel(got_ref, send_ref):
+    place = got_ref.shape[0] // (PLANES + 1)
     for z in range(PLANES):
-        send_ref[pl.ds(z * (plane + 1), plane), :] = rows[z * plane : (z + 1) * plane]
-    send_ref[pl.ds(plane, PLANES, plane + 1), :] = slots
-
-
-def turn_kernel(got_ref, send_ref):
+        send_ref[pl.ds(z * (place + 1), place), :] = got_ref[pl.ds(z, place, PLANES + 1), :]
+    slots = got_ref[pl.ds(PLANES, place, PLANES + 1), :]
+    lanes = slots.shape[1]
+    turned = jnp.concatenate([slots, jnp.zeros((lanes - place, lanes), F32)], axis=0).T
+    one, two = turned[:PLANES], turned[PLANES : 2 * PLANES]
+    send_ref[pl.ds(place, PLANES, place + 1), :] = one + pltpu.roll(two, place, 1)
+
+
+def reply_kernel(got_ref, table_ref, reply_ref):
+    place = got_ref.shape[0] // (PLANES + 1)
+    width = table_ref.shape[1] - 1
+    cells = table_ref.shape[2]
+    slots = got_ref[pl.ds(PLANES, place, PLANES + 1), :].astype(jnp.int32) - 1
+    lane = iota((place, cells), 1)
+    for z in range(PLANES):
+        first = onehot(lane == slots[:, z : z + 1])
+        second = onehot(lane == slots[:, PLANES + z : PLANES + z + 1])
+        masks = jnp.concatenate([first, first, second, second], axis=1)
+        field = table_ref[z, :width, :]
+        frac = jnp.broadcast_to(table_ref[z, width:, :], (width, cells))
+        fields = contract(masks, side_by_side(field), 1, 1)
+        fracs = contract(masks, side_by_side(frac), 1, 1)
+        means = got_ref[pl.ds(z, place, PLANES + 1), :]
+        reply_ref[pl.ds(z, place, PLANES), :] = fracs * means + (1.0 - fracs) * fields
+
+
+def merge_kernel(got_ref, table_ref, merged_ref):
+    width, cells = merged_ref.shape
     place = got_ref.shape[0] // PLANES - 1
-    for z in range(PLANES):
-        rows = got_ref[pl.ds(z * (place + 1), place), :]
-        send_ref[pl.ds(z, place, PLANES + 1), :] = rows
+    rows = jnp.concatenate(
+        [got_ref[pl.ds(z * (place + 1), place), :] for z in range(PLANES)], axis=0
+    )
     slots = got_ref[pl.ds(place, PLANES, place + 1), :]
     lanes = slots.shape[1]
     turned = jnp.concatenate([slots, jnp.zeros((lanes - PLANES, lanes), F32)], axis=0).T
-    one, two = turned[:place], turned[place : 2 * place]
-    send_ref[pl.ds(PLANES, place, PLANES + 1), :] = one + pltpu.roll(two, PLANES, 1)
-
-
-def merge_kernel(got_ref, frac_ref, field_ref, merged_ref, reply_ref):
-    width, cells = field_ref.shape
-    devices = reply_ref.shape[0]
-    place = devices // PLANES
-    rows = jnp.concatenate(
-        [got_ref[pl.ds(z, place, PLANES + 1), :] for z in range(PLANES)], axis=0
-    )
-    slots = got_ref[pl.ds(PLANES, place, PLANES + 1), :].astype(jnp.int32) - 1
+    turned = turned.astype(jnp.int32) - 1
     lane = iota((place, cells), 1)
     first, second = (
         jnp.concatenate(
-            [onehot(lane == slots[:, k + z : k + z + 1]) for z in range(PLANES)], axis=0
+            [onehot(lane == turned[k : k + place, z : z + 1]) for z in range(PLANES)], axis=0
         )
-        for k in (0, PLANES)
-    )
-    frac = frac_ref[...]
-    merged = frac * from_rows(rows, first, second) + (1.0 - frac) * field_ref[...]
-    merged_ref[...] = merged
-    masks = jnp.concatenate([first, first, second, second], axis=1)
-    reply_ref[...] = contract(masks, side_by_side(merged), 1, 1)
+        for k in (0, place)
+    )
+    field, frac = table_ref[:width, :], table_ref[width:, :]
+    merged_ref[...] = frac * from_rows(rows, first, second) + (1.0 - frac) * field
 
 
 def spread_kernel(count_ref, back_ref, first_ref, second_ref, cell_of_ref, scaled_ref, out_ref):
@@ -227,7 +254,7 @@
 SMEM = pl.BlockSpec(memory_space=pltpu.SMEM)
 
 
-def exchange(x, axis=AXES, groups=None):
+def exchange(x, axis, groups):
     return lax.all_to_all(
         x, axis, split_axis=0, concat_axis=0, tiled=True, axis_index_groups=groups
     )
@@ -257,17 +284,18 @@
     columns = lax.axis_size("clump") // PLANES
     along = [[z * columns + i for z in range(PLANES)] for i in range(columns)]
     across = [[z * place + i for i in range(place)] for z in range(PLANES)]
-    send, scaled, cell_of, first, second = pl.pallas_call(
+    send, table, scaled, cell_of, first, second = pl.pallas_call(
         gather_kernel,
         out_shape=(
-            shape((devices + PLANES, lanes), F32),
+            shape((place * (PLANES + 1), lanes), F32),
+            shape((width + 1, cells), F32),
             shape((width, patches), F32),
             shape((cells, patches), BF16),
             shape((devices, cells), BF16),
             shape((devices, cells), BF16),
         ),
-        in_specs=[SMEM] + [HBM] * 10,
-        out_specs=(VMEM,) * 5,
+        in_specs=[SMEM] + [HBM] * 12,
+        out_specs=(VMEM,) * 6,
         scratch_shapes=[
             pltpu.VMEM(col_lu.shape, jnp.int32),
             pltpu.VMEM(lu_wt.shape, F32),
@@ -279,7 +307,7 @@
             pltpu.VMEM(patch_wt.shape, F32),
             pltpu.VMEM(cell_target.shape, jnp.int32),
             pltpu.VMEM((width, patches), F32),
-            pltpu.SemaphoreType.DMA((10,)),
+            pltpu.SemaphoreType.DMA((12,)),
         ],
         compiler_params=PARAMS,
         name="gather_cells",
@@ -298,29 +326,42 @@
                 lu_grid,
                 cell_target,
                 pft_scale,
+                cpl_field.T,
+                cpl_frac.reshape(1, cells),
             )
         ),
     )
-    got = exchange(send.reshape(PLANES, 1, (place + 1) * lanes), "clump", along)
-    send = pl.pallas_call(
+    got = exchange(send.reshape(place, 1, (PLANES + 1) * lanes), AXES, across)
+    got = got.reshape(place * (PLANES + 1), lanes)
+    onward = pl.pallas_call(
         turn_kernel,
-        out_shape=shape((place * (PLANES + 1), lanes), F32),
+        out_shape=shape((PLANES * (place + 1), lanes), F32),
         in_specs=[VMEM],
         out_specs=VMEM,
         compiler_params=PARAMS,
         name="turn_rows",
-    )(got.reshape(PLANES * (place + 1), lanes))
-    got = exchange(send.reshape(place, 1, (PLANES + 1) * lanes), AXES, across)
-    got = got.reshape(place * (PLANES + 1), lanes)
-    merged, reply = pl.pallas_call(
+    )(got)
+    owned = exchange(onward.reshape(PLANES, 1, (place + 1) * lanes), "clump", along)
+    owned = owned.reshape(PLANES * (place + 1), lanes)
+    tables = lax.all_gather(table, "clump", axis=0, tiled=False, axis_index_groups=along)
+    reply = pl.pallas_call(
+        reply_kernel,
+        out_shape=shape((devices, lanes), F32),
+        in_specs=[VMEM] * 2,
+        out_specs=VMEM,
+        compiler_params=PARAMS,
+        name="reply_rows",
+    )(got, tables)
+    back = exchange(reply.reshape(place, 1, PLANES * lanes), AXES, across)
+    back = back.reshape(devices, lanes)
+    merged = pl.pallas_call(
         merge_kernel,
-        out_shape=(shape((width, cells), F32), shape((devices, 2 * width), F32)),
-        in_specs=[VMEM] * 3,
-        out_specs=(VMEM, VMEM),
+        out_shape=shape((width, cells), F32),
+        in_specs=[VMEM] * 2,
+        out_specs=VMEM,
         compiler_params=PARAMS,
         name="merge_cells",
-    )(got, cpl_frac.reshape(1, cells), cpl_field.T)
-    back = exchange(reply.reshape(devices, 1, 2 * width)).reshape(devices, 2 * width)
+    )(owned, table)
     anomaly = pl.pallas_call(
         spread_kernel,
         out_shape=shape((width, patches), F32),
@@ -334,6 +375,7 @@
 
 def solution(mesh):
     rows = P(AXES, None)
+
     return jax.shard_map(
         per_device,
         mesh=mesh,

time: 93.8 us -> 96.1 us (1.025)
  the two profiles are of different devices: /device:TPU:1 before, /device:TPU:32 now
where the time goes in v3:
time: 96.1 us; the launch traced here: 95.8 us
  blocking collectives  36.5 us (38%)
  waiting for transfers between devices  25.4 us (26%)
  starting transfers between devices  24 us (25%)
  Pallas kernels  8.45 us (9%)
  between operations  1.31 us (1%)
    all_gather x1, blocking collectives, per_device(): lax.all_gather(table, 'clump', axis=0, tiled=False, axis_index_groups=along)  36.5 us
    all_to_all x3, waiting for transfers between devices, exchange(): lax.all_to_all(x, axis, split_axis=0, concat_axis=0, tiled=True, axis_ind...  25.4 us
    all_to_all x3, starting transfers between devices, exchange(): lax.all_to_all(x, axis, split_axis=0, concat_axis=0, tiled=True, axis_ind...  24 us
    pallas_call x1, Pallas kernels, per_device(): pl.pallas_call(gather_kernel, out_shape=(shape((place * (PLANES + 1), lan...  3.2 us
    pallas_call x1, Pallas kernels, per_device(): pl.pallas_call(reply_kernel, out_shape=shape((devices, lanes), F32), in_s...  1.96 us
  transfers between devices with their start and end apart: 3, of which 2 were waited for; matrix products, arithmetic and copies ran while one was open for 0% of the time, Pallas kernels for 2%

profile of v3, /device:TPU:32, one launch (start us, length us, event | category | flops | bytes accessed | tf_op | source)
XLA Modules:
  0.0 95.8 jit_solution(14767782812897548764)
XLA Ops:
  1.3 3.2 %gather_cells.1 = (f32[544,128]{1,0:T(8,128)}, f32[65,128]{1,0:T(8,128)S(1)}, f32[64,1024]{1,0:T(8,128)S(1)}, bf16[128,1024]{1,0:T(8,128)(2,1)S(1)}, bf16[512,12...) custom-call(s32[1]{0:T(128)S(6)} %copy.18.count_ref, f32[64,1024]{1,0:T(8,128)} %bitcast.22, s32[1,1024]{1,0:T(1,128)} %pft_ref.1, ...), custom_call_target="tpu_custom_call" | custom-call | tf_op jit(solution)/shard_map/gather_cells/pallas_call | solution.py:287
  4.5 7.3 %all-to-all-start = ((f32[32,1,2176]{2,1,0:T(1,128)}), f32[32,1,2176]{2,1,0:T(1,128)S(1)}, u32[]{:S(2)}, u32[]{:S(2)}) async-start(f32[32,1,2176]{2,1,0:T(1,128)} %bitcast.4), calls=%async_computation | async-start | bytes 557056 | tf_op jit(solution)/shard_map/all_to_all | solution.py:258
  11.8 36.5 %all-gather.1.table_ref = f32[16,65,128]{2,1,0:T(8,128)S(1)} all-gather(f32[1,65,128]{2,1,0:T(8,128)S(1)} %bitcast.20), channel_id=2, replica_groups={{0,32,64,96,128,160,192,224,256,288,320,352,384,416,448,480},{4,36,68,1..., dimensions={0}, use_global_device_ids=true | all-gather | bytes 565760 | tf_op jit(solution)/shard_map/all_gather | solution.py:346
  48.4 0.0 all-to-all-done
  48.4 2.0 %reply_rows.1 = f32[512,128]{1,0:T(8,128)} custom-call(f32[544,128]{1,0:T(8,128)S(1)} %bitcast.16, f32[16,65,128]{2,1,0:T(8,128)S(1)} %all-gather.1.table_ref), custom_call_target="tpu_custom_call" | custom-call | tf_op jit(solution)/shard_map/reply_rows/pallas_call | solution.py:347
  50.3 7.5 %all-to-all-start.2 = ((f32[32,1,2048]{2,1,0:T(1,128)}), f32[32,1,2048]{2,1,0:T(1,128)S(1)}, u32[]{:S(2)}, u32[]{:S(2)}) async-start(f32[32,1,2048]{2,1,0:T(1,128)} %bitcast.10), calls=%async_computation.2 | async-start | bytes 524288 | tf_op jit(solution)/shard_map/all_to_all | solution.py:258
  57.8 0.8 turn_rows.1
  58.7 8.0 %all-to-all-done.2 = f32[32,1,2048]{2,1,0:T(1,128)S(1)} async-done(((f32[32,1,2048]{2,1,0:T(1,128)}), f32[32,1,2048]{2,1,0:T(1,128)S(1)}, u32[]{:S(2)}, u32[]{:S(2)}) %all-to-all-start.2) | async-done | bytes 262176 | tf_op jit(solution)/shard_map/all_to_all | solution.py:258
  66.7 9.2 %all-to-all-start.1 = ((f32[16,1,4224]{2,1,0:T(1,128)}), f32[16,1,4224]{2,1,0:T(1,128)S(1)}, u32[]{:S(2)}, u32[]{:S(2)}) async-start(f32[16,1,4224]{2,1,0:T(1,128)} %bitcast.6), calls=%async_computation.1 | async-start | bytes 540672 | tf_op jit(solution)/shard_map/all_to_all | solution.py:258
  75.9 1.2 %spread_cells.1 = f32[64,1024]{1,0:T(8,128)} custom-call(s32[1]{0:T(128)S(6)} %copy.18.count_ref, f32[512,128]{1,0:T(8,128)S(1)} %bitcast.19, bf16[512,128]{1,0:T(8,128)(2,1)S(1)} %get-tuple-element.10.first_ref, bf16[512,128]{1,0:T(8,128)(2,1)S(1)} %get-tuple-element.11.second_ref, bf16[128,1024]{1,0:T(8,128)(2,1)S(1)} %get-tuple-element.12.cell_of_ref, ...), custom_call_target="tpu_custom_call" | custom-call | tf_op jit(solution)/shard_map/spread_cells/pallas_call | solution.py:365
  77.2 17.4 %all-to-all-done.1 = f32[16,1,4224]{2,1,0:T(1,128)S(1)} async-done(((f32[16,1,4224]{2,1,0:T(1,128)}), f32[16,1,4224]{2,1,0:T(1,128)S(1)}, u32[]{:S(2)}, u32[]{:S(2)}) %all-to-all-start.1) | async-done | bytes 270368 | tf_op jit(solution)/shard_map/all_to_all | solution.py:258
  94.5 1.2 %merge_cells.1 = f32[64,128]{1,0:T(8,128)} custom-call(f32[528,128]{1,0:T(8,128)S(1)} %bitcast.18, f32[65,128]{1,0:T(8,128)S(1)} %get-tuple-element.9.table_ref), custom_call_target="tpu_custom_call" | custom-call | tf_op jit(solution)/shard_map/merge_cells/pallas_call | solution.py:357
Async XLA Ops:
  4.5 43.9 %all-to-all-start = ((f32[32,1,2176]{2,1,0:T(1,128)}), f32[32,1,2176]{2,1,0:T(1,128)S(1)}, u32[]{:S(2)}, u32[]{:S(2)}) async-start(f32[32,1,2176]{2,1,0:T(1,128)} %bitcast.4), calls=%async_computation | async-start | bytes 557056 | tf_op jit(solution)/shard_map/all_to_all | solution.py:258
  50.3 16.4 %all-to-all-start.2 = ((f32[32,1,2048]{2,1,0:T(1,128)}), f32[32,1,2048]{2,1,0:T(1,128)S(1)}, u32[]{:S(2)}, u32[]{:S(2)}) async-start(f32[32,1,2048]{2,1,0:T(1,128)} %bitcast.10), calls=%async_computation.2 | async-start | bytes 524288 | tf_op jit(solution)/shard_map/all_to_all | solution.py:258
  66.7 27.8 %all-to-all-start.1 = ((f32[16,1,4224]{2,1,0:T(1,128)}), f32[16,1,4224]{2,1,0:T(1,128)S(1)}, u32[]{:S(2)}, u32[]{:S(2)}) async-start(f32[16,1,4224]{2,1,0:T(1,128)} %bitcast.6), calls=%async_computation.1 | async-start | bytes 540672 | tf_op jit(solution)/shard_map/all_to_all | solution.py:258

commit v4 on v2

--- a/solution.py
+++ b/solution.py
@@ -75,7 +75,10 @@
     lu_grid_ref,
     target_ref,
     scale_ref,
+    field_ref,
+    frac_ref,
     send_ref,
+    table_ref,
     scaled_ref,
     cell_of_ref,
     first_ref,
@@ -98,7 +101,11 @@
     copies = [
         pltpu.make_async_copy(src, dst, sems.at[i]) for i, (src, dst) in enumerate(zip(given, held))
     ]
-    for copy in copies:
+    tables = [
+        pltpu.make_async_copy(field_ref, table_ref.at[pl.ds(0, field_ref.shape[0])], sems.at[10]),
+        pltpu.make_async_copy(frac_ref, table_ref.at[pl.ds(field_ref.shape[0], 1)], sems.at[11]),
+    ]
+    for copy in copies + tables:
         copy.start()
     (
         col_lu_ref,
@@ -176,6 +183,8 @@
     for z in range(PLANES):
         send_ref[pl.ds(z * (plane + 1), plane), :] = rows[z * plane : (z + 1) * plane]
     send_ref[pl.ds(plane, PLANES, plane + 1), :] = slots
+    for copy in tables:
+        copy.wait()
 
 
 def turn_kernel(got_ref, send_ref):
@@ -190,8 +199,14 @@
     send_ref[pl.ds(PLANES, place, PLANES + 1), :] = one + pltpu.roll(two, PLANES, 1)
 
 
-def merge_kernel(got_ref, frac_ref, field_ref, merged_ref, reply_ref):
-    width, cells = field_ref.shape
+def turn_back_kernel(got_ref, send_ref):
+    place = got_ref.shape[0] // PLANES
+    for z in range(PLANES):
+        send_ref[pl.ds(z * place, place), :] = got_ref[pl.ds(z, place, PLANES), :]
+
+
+def merge_kernel(got_ref, table_ref, merged_ref, reply_ref):
+    width, cells = merged_ref.shape
     devices = reply_ref.shape[0]
     place = devices // PLANES
     rows = jnp.concatenate(
@@ -205,11 +220,13 @@
         )
         for k in (0, PLANES)
     )
-    frac = frac_ref[...]
-    merged = frac * from_rows(rows, first, second) + (1.0 - frac) * field_ref[...]
+    field, frac = table_ref[:width, :], table_ref[width:, :]
+    merged = frac * from_rows(rows, first, second) + (1.0 - frac) * field
     merged_ref[...] = merged
     masks = jnp.concatenate([first, first, second, second], axis=1)
-    reply_ref[...] = contract(masks, side_by_side(merged), 1, 1)
+    rows = contract(masks, side_by_side(merged), 1, 1)
+    for z in range(PLANES):
+        reply_ref[pl.ds(z, place, PLANES), :] = rows[z * place : (z + 1) * place]
 
 
 def spread_kernel(count_ref, back_ref, first_ref, second_ref, cell_of_ref, scaled_ref, out_ref):
@@ -227,7 +244,7 @@
 SMEM = pl.BlockSpec(memory_space=pltpu.SMEM)
 
 
-def exchange(x, axis=AXES, groups=None):
+def exchange(x, axis, groups):
     return lax.all_to_all(
         x, axis, split_axis=0, concat_axis=0, tiled=True, axis_index_groups=groups
     )
@@ -257,17 +274,18 @@
     columns = lax.axis_size("clump") // PLANES
     along = [[z * columns + i for z in range(PLANES)] for i in range(columns)]
     across = [[z * place + i for i in range(place)] for z in range(PLANES)]
-    send, scaled, cell_of, first, second = pl.pallas_call(
+    send, table, scaled, cell_of, first, second = pl.pallas_call(
         gather_kernel,
         out_shape=(
             shape((devices + PLANES, lanes), F32),
+            shape((width + 1, cells), F32),
             shape((width, patches), F32),
             shape((cells, patches), BF16),
             shape((devices, cells), BF16),
             shape((devices, cells), BF16),
         ),
-        in_specs=[SMEM] + [HBM] * 10,
-        out_specs=(VMEM,) * 5,
+        in_specs=[SMEM] + [HBM] * 12,
+        out_specs=(VMEM,) * 6,
         scratch_shapes=[
             pltpu.VMEM(col_lu.shape, jnp.int32),
             pltpu.VMEM(lu_wt.shape, F32),
@@ -279,7 +297,7 @@
             pltpu.VMEM(patch_wt.shape, F32),
             pltpu.VMEM(cell_target.shape, jnp.int32),
             pltpu.VMEM((width, patches), F32),
-            pltpu.SemaphoreType.DMA((10,)),
+            pltpu.SemaphoreType.DMA((12,)),
         ],
         compiler_params=PARAMS,
         name="gather_cells",
@@ -298,6 +316,8 @@
                 lu_grid,
                 cell_target,
                 pft_scale,
+                cpl_field.T,
+                cpl_frac.reshape(1, cells),
             )
         ),
     )
@@ -315,12 +335,22 @@
     merged, reply = pl.pallas_call(
         merge_kernel,
         out_shape=(shape((width, cells), F32), shape((devices, 2 * width), F32)),
-        in_specs=[VMEM] * 3,
+        in_specs=[VMEM] * 2,
         out_specs=(VMEM, VMEM),
         compiler_params=PARAMS,
         name="merge_cells",
-    )(got, cpl_frac.reshape(1, cells), cpl_field.T)
-    back = exchange(reply.reshape(devices, 1, 2 * width)).reshape(devices, 2 * width)
+    )(got, table)
+    back = exchange(reply.reshape(place, 1, PLANES * lanes), AXES, across)
+    back = pl.pallas_call(
+        turn_back_kernel,
+        out_shape=shape((devices, lanes), F32),
+        in_specs=[VMEM],
+        out_specs=VMEM,
+        compiler_params=PARAMS,
+        name="turn_back",
+    )(back.reshape(devices, lanes))
+    back = exchange(back.reshape(PLANES, 1, place * lanes), "clump", along)
+    back = back.reshape(devices, lanes)
     anomaly = pl.pallas_call(
         spread_kernel,
         out_shape=shape((width, patches), F32),

time: 93.8 us -> 93.4 us (level)
  the two profiles are of different devices: /device:TPU:1 before, /device:TPU:32 now
where the time goes in v4:
time: 93.4 us; the launch traced here: 93.2 us
  blocking collectives  86.8 us (93%)
  Pallas kernels  5.12 us (5%)
  between operations  1.29 us (1%)
    all_to_all x4, blocking collectives, exchange(): lax.all_to_all(x, axis, split_axis=0, concat_axis=0, tiled=True, axis_ind...  86.8 us
    pallas_call x1, Pallas kernels, per_device(): pl.pallas_call(gather_kernel, out_shape=(shape((devices + PLANES, lanes),...  2.5 us

profile of v4, /device:TPU:32, one launch (start us, length us, event | category | flops | bytes accessed | tf_op | source)
XLA Modules:
  0.0 93.2 jit_solution(11812539769559702218)
XLA Ops:
  1.3 2.5 %gather_cells.1 = (f32[528,128]{1,0:T(8,128)S(1)}, f32[65,128]{1,0:T(8,128)S(1)}, f32[64,1024]{1,0:T(8,128)S(1)}, bf16[128,1024]{1,0:T(8,128)(2,1)S(1)}, bf16[51...) custom-call(s32[1]{0:T(128)S(6)} %copy.19.count_ref, f32[64,1024]{1,0:T(8,128)} %bitcast.26, s32[1,1024]{1,0:T(1,128)} %pft_ref.1, ...), custom_call_target="tpu_custom_call" | custom-call | tf_op jit(solution)/shard_map/gather_cells/pallas_call | solution.py:277
  3.8 33.0 %all_to_all.20 = f32[16,1,4224]{2,1,0:T(1,128)S(1)} all-to-all(f32[16,1,4224]{2,1,0:T(1,128)S(1)} %bitcast.23), channel_id=1, replica_groups={{0,32,64,96,128,160,192,224,256,288,320,352,384,416,448,480},{4,36,68,1..., dimensions={0} | all-to-all | bytes 540672 | tf_op jit(solution)/shard_map/all_to_all | solution.py:248
  36.8 0.1 turn_rows.1
  36.9 16.2 %all_to_all.21 = f32[32,1,2176]{2,1,0:T(1,128)S(1)} all-to-all(f32[32,1,2176]{2,1,0:T(1,128)S(1)} %bitcast.18), channel_id=1, replica_groups={{0,1,2,3,4,5,6,7,8,9,10,11,12,13,14,15,16,17,18,19,20,21,22,23,24,25,26..., dimensions={0} | all-to-all | bytes 557056 | tf_op jit(solution)/shard_map/all_to_all | solution.py:248
  53.1 1.2 %merge_cells.1 = (f32[64,128]{1,0:T(8,128)}, f32[512,128]{1,0:T(8,128)S(1)}) custom-call(f32[544,128]{1,0:T(8,128)S(1)} %bitcast.17, f32[65,128]{1,0:T(8,128)S(1)} %get-tuple-element.11.table_ref), custom_call_target="tpu_custom_call" | custom-call | tf_op jit(solution)/shard_map/merge_cells/pallas_call | solution.py:335
  54.3 12.8 %all_to_all.22 = f32[32,1,2048]{2,1,0:T(1,128)S(1)} all-to-all(f32[32,1,2048]{2,1,0:T(1,128)S(1)} %bitcast.24), channel_id=1, replica_groups={{0,1,2,3,4,5,6,7,8,9,10,11,12,13,14,15,16,17,18,19,20,21,22,23,24,25,26..., dimensions={0} | all-to-all | bytes 524288 | tf_op jit(solution)/shard_map/all_to_all | solution.py:248
  67.1 0.1 turn_back.1
  67.2 24.7 %all_to_all.23 = f32[16,1,4096]{2,1,0:T(1,128)S(1)} all-to-all(f32[16,1,4096]{2,1,0:T(1,128)S(1)} %bitcast.22), channel_id=1, replica_groups={{0,32,64,96,128,160,192,224,256,288,320,352,384,416,448,480},{4,36,68,1..., dimensions={0} | all-to-all | bytes 524288 | tf_op jit(solution)/shard_map/all_to_all | solution.py:248
  91.9 1.2 %spread_cells.1 = f32[64,1024]{1,0:T(8,128)} custom-call(s32[1]{0:T(128)S(6)} %copy.19.count_ref, f32[512,128]{1,0:T(8,128)S(1)} %bitcast.20, bf16[512,128]{1,0:T(8,128)(2,1)S(1)} %get-tuple-element.14.first_ref, bf16[512,128]{1,0:T(8,128)(2,1)S(1)} %get-tuple-element.15.second_ref, bf16[128,1024]{1,0:T(8,128)(2,1)S(1)} %get-tuple-element.16.cell_of_ref, ...), custom_call_target="tpu_custom_call" | custom-call | tf_op jit(solution)/shard_map/spread_cells/pallas_call | solution.py:354

commit v5 on v4

--- a/solution.py
+++ b/solution.py
@@ -39,8 +39,12 @@
     return jnp.max(jnp.where(same & earlier, F32(1.0), F32(0.0)), axis=0, keepdims=True)
 
 
+def ordered(owner):
+    return owner // 8 * 8 + owner % 4 * 2 + owner // 4 % 2
+
+
 def pair_masks(target, cells, devices):
-    owner = target // cells
+    owner = ordered(target // cells)
     rank = earlier_mate(owner, cells)
     hit = iota((devices, cells), 0) == owner
     return onehot(hit & (rank < 0.5)), onehot(hit & (rank > 0.5))
@@ -174,7 +178,7 @@
     plane = devices // PLANES
     target = target_ref[...]
     slot = (target % cells + 1).astype(F32)
-    owner = target // cells
+    owner = ordered(target // cells)
     rank = earlier_mate(owner, cells)
     lane = owner % plane + jnp.where(rank > 0.5, plane, 0)
     left = jnp.where(iota((PLANES, cells), 0) == owner // plane, slot, F32(0.0)).astype(BF16)
@@ -200,33 +204,30 @@
 
 
 def turn_back_kernel(got_ref, send_ref):
-    place = got_ref.shape[0] // PLANES
-    for z in range(PLANES):
-        send_ref[pl.ds(z * place, place), :] = got_ref[pl.ds(z, place, PLANES), :]
+    chips = got_ref.shape[0] // 2
+    for core in range(2):
+        send_ref[pl.ds(core, chips, 2), :] = got_ref[pl.ds(core * chips, chips), :]
 
 
 def merge_kernel(got_ref, table_ref, merged_ref, reply_ref):
     width, cells = merged_ref.shape
     devices = reply_ref.shape[0]
-    place = devices // PLANES
-    rows = jnp.concatenate(
-        [got_ref[pl.ds(z, place, PLANES + 1), :] for z in range(PLANES)], axis=0
-    )
-    slots = got_ref[pl.ds(PLANES, place, PLANES + 1), :].astype(jnp.int32) - 1
-    lane = iota((place, cells), 1)
-    first, second = (
-        jnp.concatenate(
-            [onehot(lane == slots[:, k + z : k + z + 1]) for z in range(PLANES)], axis=0
-        )
-        for k in (0, PLANES)
-    )
+    half = devices // PLANES // 2
+    step = PLANES + 1
+    lane = iota((half, cells), 1)
+    rows, first, second = [], [], []
+    for core in range(2):
+        slots = got_ref[pl.ds(core * step + PLANES, half, 2 * step), :].astype(jnp.int32) - 1
+        for z in range(PLANES):
+            rows.append(got_ref[pl.ds(core * step + z, half, 2 * step), :])
+            first.append(onehot(lane == slots[:, z : z + 1]))
+            second.append(onehot(lane == slots[:, PLANES + z : PLANES + z + 1]))
+    rows, first, second = (jnp.concatenate(x, axis=0) for x in (rows, first, second))
     field, frac = table_ref[:width, :], table_ref[width:, :]
     merged = frac * from_rows(rows, first, second) + (1.0 - frac) * field
     merged_ref[...] = merged
     masks = jnp.concatenate([first, first, second, second], axis=1)
-    rows = contract(masks, side_by_side(merged), 1, 1)
-    for z in range(PLANES):
-        reply_ref[pl.ds(z, place, PLANES), :] = rows[z * place : (z + 1) * place]
+    reply_ref[...] = contract(masks, side_by_side(merged), 1, 1)
 
 
 def spread_kernel(count_ref, back_ref, first_ref, second_ref, cell_of_ref, scaled_ref, out_ref):
@@ -273,7 +274,12 @@
     place = devices // PLANES
     columns = lax.axis_size("clump") // PLANES
     along = [[z * columns + i for z in range(PLANES)] for i in range(columns)]
-    across = [[z * place + i for i in range(place)] for z in range(PLANES)]
+    inner = [y * 8 + core * 4 + x for y in range(4) for x in range(4) for core in range(2)]
+    across = [[z * place + i for i in inner] for z in range(PLANES)]
+    chips = [
+        [z * place + i for z in range(PLANES) for i in inner[core::2]] for core in range(2)
+    ]
+    cores = [[2 * i, 2 * i + 1] for i in range(lax.axis_size("clump") // 2)]
     send, table, scaled, cell_of, first, second = pl.pallas_call(
         gather_kernel,
         out_shape=(
@@ -340,7 +346,7 @@
         compiler_params=PARAMS,
         name="merge_cells",
     )(got, table)
-    back = exchange(reply.reshape(place, 1, PLANES * lanes), AXES, across)
+    back = exchange(reply.reshape(2, devices // 2, lanes), "clump", cores)
     back = pl.pallas_call(
         turn_back_kernel,
         out_shape=shape((devices, lanes), F32),
@@ -349,7 +355,7 @@
         compiler_params=PARAMS,
         name="turn_back",
     )(back.reshape(devices, lanes))
-    back = exchange(back.reshape(PLANES, 1, place * lanes), "clump", along)
+    back = exchange(back.reshape(devices // 2, 2, lanes), AXES, chips)
     back = back.reshape(devices, lanes)
     anomaly = pl.pallas_call(
         spread_kernel,

time: 93.4 us -> 94.9 us (1.016)
  the two profiles are of different devices: /device:TPU:32 before, /device:TPU:1 now
where the time goes in v5:
time: 94.9 us; the launch traced here: 93.9 us
  blocking collectives  87.6 us (92%)
  Pallas kernels  5.06 us (5%)
  between operations  1.29 us (1%)
    all_to_all x4, blocking collectives, exchange(): lax.all_to_all(x, axis, split_axis=0, concat_axis=0, tiled=True, axis_ind...  87.6 us
    pallas_call x1, Pallas kernels, per_device(): pl.pallas_call(gather_kernel, out_shape=(shape((devices + PLANES, lanes),...  2.52 us

profile of v5, /device:TPU:1, one launch (start us, length us, event | category | flops | bytes accessed | tf_op | source)
XLA Modules:
  0.0 93.9 jit_solution(12451372585459667558)
XLA Ops:
  1.3 2.5 %gather_cells.1 = (f32[528,128]{1,0:T(8,128)S(1)}, f32[65,128]{1,0:T(8,128)S(1)}, f32[64,1024]{1,0:T(8,128)S(1)}, bf16[128,1024]{1,0:T(8,128)(2,1)S(1)}, bf16[51...) custom-call(s32[1]{0:T(128)S(6)} %copy.17.count_ref, f32[64,1024]{1,0:T(8,128)} %bitcast.26, s32[1,1024]{1,0:T(1,128)} %pft_ref.1, ...), custom_call_target="tpu_custom_call" | custom-call | tf_op jit(solution)/shard_map/gather_cells/pallas_call | solution.py:283
  3.8 29.4 %all_to_all.20 = f32[16,1,4224]{2,1,0:T(1,128)S(1)} all-to-all(f32[16,1,4224]{2,1,0:T(1,128)S(1)} %bitcast.23), channel_id=1, replica_groups={{0,32,64,96,128,160,192,224,256,288,320,352,384,416,448,480},{4,36,68,1..., dimensions={0} | all-to-all | bytes 540672 | tf_op jit(solution)/shard_map/all_to_all | solution.py:249
  33.2 0.1 turn_rows.1
  33.3 21.7 %all_to_all.21 = f32[32,1,2176]{2,1,0:T(1,128)S(1)} all-to-all(f32[32,1,2176]{2,1,0:T(1,128)S(1)} %bitcast.18), channel_id=1, replica_groups={{0,4,1,5,2,6,3,7,8,12,9,13,10,14,11,15,16,20,17,21,18,22,19,23,24,28,25..., dimensions={0} | all-to-all | bytes 557056 | tf_op jit(solution)/shard_map/all_to_all | solution.py:249
  55.0 1.2 %merge_cells.1 = (f32[64,128]{1,0:T(8,128)}, f32[512,128]{1,0:T(8,128)S(1)}) custom-call(f32[544,128]{1,0:T(8,128)S(1)} %bitcast.17, f32[65,128]{1,0:T(8,128)S(1)} %get-tuple-element.11.table_ref), custom_call_target="tpu_custom_call" | custom-call | tf_op jit(solution)/shard_map/merge_cells/pallas_call | solution.py:341
  56.2 3.7 %all_to_all.22 = f32[2,256,128]{2,1,0:T(8,128)S(1)} all-to-all(f32[2,256,128]{2,1,0:T(8,128)S(1)} %bitcast.24), channel_id=1, replica_groups={{0,4},{8,12},{16,20},{24,28},{32,36},{40,44},{48,52},{56,60},{64,68},{7..., dimensions={0} | all-to-all | bytes 524288 | tf_op jit(solution)/shard_map/all_to_all | solution.py:249
  60.0 32.7 %all_to_all.23 = f32[256,2,128]{2,1,0:T(2,128)S(1)} all-to-all(f32[256,2,128]{2,1,0:T(2,128)S(1)} %bitcast.22), channel_id=1, replica_groups={{0,1,2,3,8,9,10,11,16,17,18,19,24,25,26,27,32,33,34,35,40,41,42,43,48,4..., dimensions={0} | all-to-all | bytes 524288 | tf_op jit(solution)/shard_map/all_to_all | solution.py:249
  92.7 1.2 %spread_cells.1 = f32[64,1024]{1,0:T(8,128)} custom-call(s32[1]{0:T(128)S(6)} %copy.17.count_ref, f32[512,128]{1,0:T(8,128)S(1)} %bitcast.20, bf16[512,128]{1,0:T(8,128)(2,1)S(1)} %get-tuple-element.14.first_ref, bf16[512,128]{1,0:T(8,128)(2,1)S(1)} %get-tuple-element.15.second_ref, bf16[128,1024]{1,0:T(8,128)(2,1)S(1)} %get-tuple-element.16.cell_of_ref, ...), custom_call_target="tpu_custom_call" | custom-call | tf_op jit(solution)/shard_map/spread_cells/pallas_call | solution.py:360
  (1 shorter events, 0.0 us)

commit v6 on v4

--- a/solution.py
+++ b/solution.py
@@ -1,3 +1,5 @@
+import functools
+
 import jax
 import jax.numpy as jnp
 from jax import lax
@@ -32,18 +34,17 @@
     return lax.broadcasted_iota(jnp.int32, shape, dim)
 
 
-def earlier_mate(owner, cells):
-    owner_rows = jnp.broadcast_to(owner, (cells, cells)).astype(F32)
-    same = owner_rows.T == owner_rows
-    earlier = iota((cells, cells), 0) < iota((cells, cells), 1)
-    return jnp.max(jnp.where(same & earlier, F32(1.0), F32(0.0)), axis=0, keepdims=True)
-
-
-def pair_masks(target, cells, devices):
+def cell_rows(target, cells, devices):
+    place = devices // PLANES
     owner = target // cells
-    rank = earlier_mate(owner, cells)
-    hit = iota((devices, cells), 0) == owner
-    return onehot(hit & (rank < 0.5)), onehot(hit & (rank > 0.5))
+    across = jnp.broadcast_to(owner, (cells, cells)).astype(F32)
+    down = across.T
+    base = jnp.broadcast_to(owner - owner % place, (cells, cells)).astype(F32)
+    earlier = (down == across) & (iota((cells, cells), 0) < iota((cells, cells), 1))
+    rank = jnp.max(jnp.where(earlier, F32(1.0), F32(0.0)), axis=0, keepdims=True)
+    below = (down < across) & (down >= base)
+    row = jnp.sum(jnp.where(below, F32(0.5), F32(0.0)), axis=0, keepdims=True)
+    return owner // place, owner % place, rank > 0.5, row.astype(jnp.int32)
 
 
 def side_by_side(x):
@@ -64,6 +65,7 @@
 
 
 def gather_kernel(
+    devices,
     count_ref,
     flux_ref,
     pft_ref,
@@ -123,7 +125,8 @@
         copy.wait()
     width, patches = flux_ref.shape
     cells = target_ref.shape[1]
-    devices = send_ref.shape[0] - PLANES
+    room = send_ref.shape[0] // PLANES - 1
+    lanes = send_ref.shape[1]
     columns = col_wt_ref.shape[1]
     units = lu_wt_ref.shape[1]
     types = scale_ref.shape[0]
@@ -166,46 +169,75 @@
     mean = total[:width] / jnp.maximum(total[width : width + 1], 1.0)
 
     copies[8].wait()
-    first, second = pair_masks(target_ref[...], cells, devices)
-    first_ref[...] = first
-    second_ref[...] = second
-    masks = jnp.concatenate([first, first, second, second], axis=1)
-    rows = contract(masks, side_by_side(mean), 1, 1)
-    plane = devices // PLANES
     target = target_ref[...]
+    plane, place, second, row = cell_rows(target, cells, devices)
+    hit = iota((PLANES * room, cells), 0) == plane * room + row
+    one, two = onehot(hit & jnp.logical_not(second)), onehot(hit & second)
+    first_ref[...] = one
+    second_ref[...] = two
+    rows = contract(jnp.concatenate([one, one, two, two], axis=1), side_by_side(mean), 1, 1)
+
+    in_plane = iota((PLANES, cells), 0) == plane
     slot = (target % cells + 1).astype(F32)
-    owner = target // cells
-    rank = earlier_mate(owner, cells)
-    lane = owner % plane + jnp.where(rank > 0.5, plane, 0)
-    left = jnp.where(iota((PLANES, cells), 0) == owner // plane, slot, F32(0.0)).astype(BF16)
-    right = onehot(iota((2 * width, cells), 0) == lane)
-    slots = contract(left, right, 1, 1)
+    seat = jnp.where(second, F32(0.0), (place + 1).astype(F32))
+    left = jnp.concatenate(
+        [jnp.where(in_plane, seat, F32(0.0)), jnp.where(in_plane, slot, F32(0.0))], axis=1
+    ).astype(BF16)
+    lane = iota((lanes, cells), 0)
+    right = jnp.concatenate(
+        [onehot(lane == row), onehot(lane == row + jnp.where(second, 2 * room, room))], axis=1
+    )
+    notes = contract(left, right, 1, 1)
+    full = jnp.where(jnp.max(row, axis=1, keepdims=True) < room, F32(0.0), F32(1.0))
+    notes = jnp.where(iota((PLANES, lanes), 1) == lanes - 1, full, notes)
     for z in range(PLANES):
-        send_ref[pl.ds(z * (plane + 1), plane), :] = rows[z * plane : (z + 1) * plane]
-    send_ref[pl.ds(plane, PLANES, plane + 1), :] = slots
+        send_ref[pl.ds(z * (room + 1), room), :] = rows[z * room : (z + 1) * room]
+    send_ref[pl.ds(room, PLANES, room + 1), :] = notes
     for copy in tables:
         copy.wait()
 
 
+def seats(notes, z, place, room):
+    return onehot(iota((place, room), 0) == notes[z : z + 1, :room].astype(jnp.int32) - 1)
+
+
 def turn_kernel(got_ref, send_ref):
-    place = got_ref.shape[0] // PLANES - 1
+    room = got_ref.shape[0] // PLANES - 1
+    place = send_ref.shape[0] // (PLANES + 1)
+    lanes = got_ref.shape[1]
+    notes = got_ref[pl.ds(room, PLANES, room + 1), :]
+    turned = jnp.concatenate([notes, jnp.zeros((lanes - PLANES, lanes), F32)], axis=0).T
+    slots = turned[room : 2 * room] + pltpu.roll(turned[2 * room : 3 * room], PLANES, 1)
+    lane = iota((room, lanes), 1)
+    picks, parts = [], []
     for z in range(PLANES):
-        rows = got_ref[pl.ds(z * (place + 1), place), :]
-        send_ref[pl.ds(z, place, PLANES + 1), :] = rows
-    slots = got_ref[pl.ds(place, PLANES, place + 1), :]
-    lanes = slots.shape[1]
-    turned = jnp.concatenate([slots, jnp.zeros((lanes - PLANES, lanes), F32)], axis=0).T
-    one, two = turned[:place], turned[place : 2 * place]
-    send_ref[pl.ds(PLANES, place, PLANES + 1), :] = one + pltpu.roll(two, PLANES, 1)
-
-
-def turn_back_kernel(got_ref, send_ref):
-    place = got_ref.shape[0] // PLANES
+        pick = seats(notes, z, place, room)
+        hi, lo = pieces(got_ref[pl.ds(z * (room + 1), room), :], 2)
+        send_ref[pl.ds(z, place, PLANES + 1), :] = contract(
+            jnp.concatenate([pick, pick], axis=1), jnp.concatenate([hi, lo], axis=0), 1, 0
+        )
+        picks.append(pick)
+        mine = (lane == z) | (lane == PLANES + z)
+        parts.append(jnp.where(mine, slots, F32(0.0)).astype(BF16))
+    passed = contract(jnp.concatenate(picks, axis=1), jnp.concatenate(parts, axis=0), 1, 0)
+    full = jnp.max(notes[:, lanes - 1 :], axis=0, keepdims=True)
+    passed = jnp.where(iota((place, lanes), 1) == lanes - 1, full, passed)
+    send_ref[pl.ds(PLANES, place, PLANES + 1), :] = passed
+
+
+def turn_back_kernel(got_ref, back_ref, send_ref):
+    room = got_ref.shape[0] // PLANES - 1
+    place = back_ref.shape[0] // PLANES
+    notes = got_ref[pl.ds(room, PLANES, room + 1), :]
     for z in range(PLANES):
-        send_ref[pl.ds(z * place, place), :] = got_ref[pl.ds(z, place, PLANES), :]
-
-
-def merge_kernel(got_ref, table_ref, merged_ref, reply_ref):
+        pick = seats(notes, z, place, room)
+        hi, lo = pieces(back_ref[pl.ds(z, place, PLANES), :], 2)
+        send_ref[pl.ds(z * room, room), :] = contract(
+            jnp.concatenate([pick, pick], axis=0), jnp.concatenate([hi, lo], axis=0), 0, 0
+        )
+
+
+def merge_kernel(got_ref, table_ref, merged_ref, reply_ref, full_ref):
     width, cells = merged_ref.shape
     devices = reply_ref.shape[0]
     place = devices // PLANES
@@ -213,6 +245,7 @@
         [got_ref[pl.ds(z, place, PLANES + 1), :] for z in range(PLANES)], axis=0
     )
     slots = got_ref[pl.ds(PLANES, place, PLANES + 1), :].astype(jnp.int32) - 1
+    full_ref[0] = jnp.max(slots[:, slots.shape[1] - 1 :]) + 1
     lane = iota((place, cells), 1)
     first, second = (
         jnp.concatenate(
@@ -250,7 +283,8 @@
     )
 
 
-def per_device(
+def pipeline(
+    room,
     flux,
     patch_pft,
     patch_wt,
@@ -275,14 +309,14 @@
     along = [[z * columns + i for z in range(PLANES)] for i in range(columns)]
     across = [[z * place + i for i in range(place)] for z in range(PLANES)]
     send, table, scaled, cell_of, first, second = pl.pallas_call(
-        gather_kernel,
+        functools.partial(gather_kernel, devices),
         out_shape=(
-            shape((devices + PLANES, lanes), F32),
+            shape((PLANES * (room + 1), lanes), F32),
             shape((width + 1, cells), F32),
             shape((width, patches), F32),
             shape((cells, patches), BF16),
-            shape((devices, cells), BF16),
-            shape((devices, cells), BF16),
+            shape((PLANES * room, cells), BF16),
+            shape((PLANES * room, cells), BF16),
         ),
         in_specs=[SMEM] + [HBM] * 12,
         out_specs=(VMEM,) * 6,
@@ -321,7 +355,8 @@
             )
         ),
     )
-    got = exchange(send.reshape(PLANES, 1, (place + 1) * lanes), "clump", along)
+    noted = exchange(send.reshape(PLANES, 1, (room + 1) * lanes), "clump", along)
+    noted = noted.reshape(PLANES * (room + 1), lanes)
     send = pl.pallas_call(
         turn_kernel,
         out_shape=shape((place * (PLANES + 1), lanes), F32),
@@ -329,28 +364,31 @@
         out_specs=VMEM,
         compiler_params=PARAMS,
         name="turn_rows",
-    )(got.reshape(PLANES * (place + 1), lanes))
+    )(noted)
     got = exchange(send.reshape(place, 1, (PLANES + 1) * lanes), AXES, across)
-    got = got.reshape(place * (PLANES + 1), lanes)
-    merged, reply = pl.pallas_call(
+    merged, reply, full = pl.pallas_call(
         merge_kernel,
-        out_shape=(shape((width, cells), F32), shape((devices, 2 * width), F32)),
+        out_shape=(
+            shape((width, cells), F32),
+            shape((devices, lanes), F32),
+            shape((1,), jnp.int32),
+        ),
         in_specs=[VMEM] * 2,
-        out_specs=(VMEM, VMEM),
+        out_specs=(VMEM, VMEM, SMEM),
         compiler_params=PARAMS,
         name="merge_cells",
-    )(got, table)
+    )(got.reshape(place * (PLANES + 1), lanes), table)
     back = exchange(reply.reshape(place, 1, PLANES * lanes), AXES, across)
     back = pl.pallas_call(
         turn_back_kernel,
-        out_shape=shape((devices, lanes), F32),
-        in_specs=[VMEM],
+        out_shape=shape((PLANES * room, lanes), F32),
+        in_specs=[VMEM] * 2,
         out_specs=VMEM,
         compiler_params=PARAMS,
         name="turn_back",
-    )(back.reshape(devices, lanes))
-    back = exchange(back.reshape(PLANES, 1, place * lanes), "clump", along)
-    back = back.reshape(devices, lanes)
+    )(noted, back.reshape(devices, lanes))
+    back = exchange(back.reshape(PLANES, 1, room * lanes), "clump", along)
+    back = back.reshape(PLANES * room, lanes)
     anomaly = pl.pallas_call(
         spread_kernel,
         out_shape=shape((width, patches), F32),
@@ -359,6 +397,20 @@
         compiler_params=PARAMS,
         name="spread_cells",
     )(patch_count, back, first, second, cell_of, scaled)
+    return merged, anomaly, full[0]
+
+
+def per_device(*args):
+    devices = lax.axis_size("clump") * lax.axis_size("grp")
+    most = devices // PLANES
+
+    def again(state):
+        merged, anomaly, _ = pipeline(most, *args)
+        return merged, anomaly, jnp.int32(0)
+
+    merged, anomaly, _ = lax.while_loop(
+        lambda state: state[2] > 0, again, pipeline(most // 2, *args)
+    )
     return merged.T, anomaly.T[None]
 
 

time: 93.4 us -> 84.1 us (0.900)
  the two profiles are of different devices: /device:TPU:32 before, /device:TPU:1 now
where the time goes in v6:
time: 84.1 us; the launch traced here: 83 us
  blocking collectives  75.8 us (90%)
  Pallas kernels  5.37 us (6%)
  between operations  1.3 us (2%)
    all_to_all x4, blocking collectives, exchange(): lax.all_to_all(x, axis, split_axis=0, concat_axis=0, tiled=True, axis_ind...  75.8 us
    pallas_call x1, Pallas kernels, pipeline(): pl.pallas_call(functools.partial(gather_kernel, devices), out_shape=(shap...  2.46 us

profile of v6, /device:TPU:1, one launch (start us, length us, event | category | flops | bytes accessed | tf_op | source)
XLA Modules:
  0.0 83.0 jit_solution(12355902064173074030)
XLA Ops:
  1.3 2.5 %gather_cells.3 = (f32[272,128]{1,0:T(8,128)S(1)}, f32[65,128]{1,0:T(8,128)S(1)}, f32[64,1024]{1,0:T(8,128)S(1)}, bf16[128,1024]{1,0:T(8,128)(2,1)S(1)}, bf16[25...) custom-call(s32[1]{0:T(128)S(6)} %copy.33.count_ref, f32[64,1024]{1,0:T(8,128)} %bitcast.48, s32[1,1024]{1,0:T(1,128)} %pft_ref.1, ...), custom_call_target="tpu_custom_call" | custom-call | tf_op jit(solution)/shard_map/gather_cells/pallas_call | solution.py:311
  3.7 27.5 %all_to_all.39 = f32[16,1,2176]{2,1,0:T(1,128)S(1)} all-to-all(f32[16,1,2176]{2,1,0:T(1,128)S(1)} %bitcast.47), channel_id=1, replica_groups={{0,32,64,96,128,160,192,224,256,288,320,352,384,416,448,480},{4,36,68,1..., dimensions={0} | all-to-all | bytes 278528 | tf_op jit(solution)/shard_map/all_to_all | solution.py:281
  31.3 0.3 turn_rows.3
  31.6 19.8 %all_to_all.40 = f32[32,1,2176]{2,1,0:T(1,128)S(1)} all-to-all(f32[32,1,2176]{2,1,0:T(1,128)S(1)} %bitcast.42), channel_id=1, replica_groups={{0,1,2,3,4,5,6,7,8,9,10,11,12,13,14,15,16,17,18,19,20,21,22,23,24,25,26..., dimensions={0} | all-to-all | bytes 557056 | tf_op jit(solution)/shard_map/all_to_all | solution.py:281
  51.4 1.2 %merge_cells.3 = (f32[64,128]{1,0:T(8,128)}, f32[512,128]{1,0:T(8,128)S(1)}, s32[1]{0:T(128)}) custom-call(f32[544,128]{1,0:T(8,128)S(1)} %bitcast.41, f32[65,128]{1,0:T(8,128)S(1)} %get-tuple-element.100.table_ref), custom_call_target="tpu_custom_call" | custom-call | tf_op jit(solution)/shard_map/merge_cells/pallas_call | solution.py:369
  52.6 12.8 %all_to_all.41 = f32[32,1,2048]{2,1,0:T(1,128)S(1)} all-to-all(f32[32,1,2048]{2,1,0:T(1,128)S(1)} %bitcast.46), channel_id=1, replica_groups={{0,1,2,3,4,5,6,7,8,9,10,11,12,13,14,15,16,17,18,19,20,21,22,23,24,25,26..., dimensions={0} | all-to-all | bytes 524288 | tf_op jit(solution)/shard_map/all_to_all | solution.py:281
  65.4 0.2 turn_back.3
  65.6 15.7 %all_to_all.42 = f32[16,1,2048]{2,1,0:T(1,128)S(1)} all-to-all(f32[16,1,2048]{2,1,0:T(1,128)S(1)} %bitcast.44), channel_id=1, replica_groups={{0,32,64,96,128,160,192,224,256,288,320,352,384,416,448,480},{4,36,68,1..., dimensions={0} | all-to-all | bytes 262144 | tf_op jit(solution)/shard_map/all_to_all | solution.py:281
  81.3 1.2 %spread_cells.3 = f32[64,1024]{1,0:T(8,128)} custom-call(s32[1]{0:T(128)S(6)} %copy.33.count_ref, f32[256,128]{1,0:T(8,128)S(1)} %bitcast.45, bf16[256,128]{1,0:T(8,128)(2,1)S(1)} %get-tuple-element.103.first_ref, bf16[256,128]{1,0:T(8,128)(2,1)S(1)} %get-tuple-element.104.second_ref, bf16[128,1024]{1,0:T(8,128)(2,1)S(1)} %get-tuple-element.105.cell_of_ref, ...), custom_call_target="tpu_custom_call" | custom-call | tf_op jit(solution)/shard_map/spread_cells/pallas_call | solution.py:392
  82.5 0.6 while.11

commit v7 on v6

--- a/solution.py
+++ b/solution.py
@@ -58,10 +58,15 @@
 
 def from_rows(rows, first, second):
     width = rows.shape[1] // 2
-    hi, lo = pieces(rows, 2)
-    one = contract(hi, first, 0, 0) + contract(lo, first, 0, 0)
-    two = contract(hi, second, 0, 0) + contract(lo, second, 0, 0)
-    return one[:width] + two[width:]
+    hi = rows.astype(BF16).astype(F32)
+    lo = rows - hi
+    left = iota(rows.shape, 1) < width
+    one = jnp.where(left, hi, pltpu.roll(lo, width, 1)).astype(BF16)
+    two = jnp.where(left, pltpu.roll(hi, width, 1), lo).astype(BF16)
+    both = contract(
+        jnp.concatenate([one, two], axis=0), jnp.concatenate([first, second], axis=0), 0, 0
+    )
+    return both[:width] + both[width:]
 
 
 def gather_kernel(
@@ -121,7 +126,7 @@
         target_ref,
         flux_ref,
     ) = held
-    for copy in copies[:4]:
+    for copy in copies[:9]:
         copy.wait()
     width, patches = flux_ref.shape
     cells = target_ref.shape[1]
@@ -142,33 +147,36 @@
     col_table = jnp.concatenate(
         pieces(col_weight, 3) + [picked[3:4].astype(BF16), jnp.zeros((12, columns), BF16)], axis=0
     )
-    copies[4].wait()
-    col_of = onehot(iota((columns, patches), 0) == col_ref[...])
-    picked = contract(col_table, col_of, 1, 0)
+    parts = []
+    span = patches // 4
+    for block in range(4):
+        start = block * span
+        low = max(start // 4, start - columns) // 128 * 128
+        high = min(start + span, columns // 2 + start // 4 + span // 4, columns)
+        high = -(-high // 128) * 128
+        here = iota((high - low, span), 0) + low == col_ref[:, start : start + span]
+        parts.append(contract(col_table[:, low:high], onehot(here), 1, 0))
+    picked = jnp.concatenate(parts, axis=1)
     alive = iota((1, patches), 1) < count_ref[0]
-    copies[7].wait()
     weight = jnp.where(
         alive, wt_ref[...] * (picked[0:1] + picked[1:2] + picked[2:3]), F32(0.0)
     )
     home = picked[3:4].astype(jnp.int32)
 
-    copies[5].wait()
-    copies[6].wait()
     type_of = onehot(iota((types, patches), 0) == pft_ref[...])
     scale_parts = jnp.concatenate(pieces(scale_ref[...], 3), axis=0)
     factor = contract(scale_parts, jnp.concatenate([type_of] * 3, axis=0), 0, 0)
     copies[9].wait()
     scaled = flux_ref[...] * factor
-    scaled_ref[...] = scaled
-
-    cell_of = onehot(iota((cells, patches), 0) == home)
+    scaled_ref[...] = jnp.where(alive, scaled, F32(0.0))
+
+    cell_of = onehot((iota((cells, patches), 0) == home) & alive)
     cell_of_ref[...] = cell_of
     terms = jnp.concatenate([scaled * weight, weight, jnp.zeros((15, patches), F32)], axis=0)
     sums = [contract(part, cell_of, 1, 1) for part in pieces(terms, 2)]
     total = sums[0] + sums[1]
     mean = total[:width] / jnp.maximum(total[width : width + 1], 1.0)
 
-    copies[8].wait()
     target = target_ref[...]
     plane, place, second, row = cell_rows(target, cells, devices)
     hit = iota((PLANES * room, cells), 0) == plane * room + row
@@ -237,15 +245,20 @@
         )
 
 
-def merge_kernel(got_ref, table_ref, merged_ref, reply_ref, full_ref):
-    width, cells = merged_ref.shape
+def merge_kernel(got_ref, table_ref, merged_ref, reply_ref, full_ref, held_ref, flag_ref, sems):
+    width, cells = held_ref.shape
     devices = reply_ref.shape[0]
     place = devices // PLANES
     rows = jnp.concatenate(
         [got_ref[pl.ds(z, place, PLANES + 1), :] for z in range(PLANES)], axis=0
     )
     slots = got_ref[pl.ds(PLANES, place, PLANES + 1), :].astype(jnp.int32) - 1
-    full_ref[0] = jnp.max(slots[:, slots.shape[1] - 1 :]) + 1
+    flag_ref[0] = jnp.max(slots[:, slots.shape[1] - 1 :]) + 1
+    copies = (
+        pltpu.make_async_copy(flag_ref, full_ref, sems.at[0]),
+        pltpu.make_async_copy(held_ref, merged_ref, sems.at[1]),
+    )
+    copies[0].start()
     lane = iota((place, cells), 1)
     first, second = (
         jnp.concatenate(
@@ -255,26 +268,41 @@
     )
     field, frac = table_ref[:width, :], table_ref[width:, :]
     merged = frac * from_rows(rows, first, second) + (1.0 - frac) * field
-    merged_ref[...] = merged
+    held_ref[...] = merged
+    copies[1].start()
     masks = jnp.concatenate([first, first, second, second], axis=1)
     rows = contract(masks, side_by_side(merged), 1, 1)
     for z in range(PLANES):
         reply_ref[pl.ds(z, place, PLANES), :] = rows[z * place : (z + 1) * place]
-
-
-def spread_kernel(count_ref, back_ref, first_ref, second_ref, cell_of_ref, scaled_ref, out_ref):
+    for copy in copies:
+        copy.wait()
+
+
+def spread_kernel(
+    back_ref, first_ref, second_ref, cell_of_ref, scaled_ref, out_ref, held_ref, sems
+):
     width, patches = scaled_ref.shape
     merged = from_rows(back_ref[...], first_ref[...], second_ref[...])
-    parts = contract(jnp.concatenate(pieces(merged, 2), axis=0), cell_of_ref[...], 1, 0)
-    picked = parts[:width] + parts[width:]
-    alive = iota((1, patches), 1) < count_ref[0]
-    out_ref[...] = jnp.where(alive, scaled_ref[...] - picked, F32(0.0))
+    both = jnp.concatenate(pieces(merged, 2), axis=0)
+    chunk = patches // 4
+    copies = []
+    for i in range(4):
+        here = pl.ds(i * chunk, chunk)
+        parts = contract(both, cell_of_ref[:, here], 1, 0)
+        held_ref[:, here] = scaled_ref[:, here] - (parts[:width] + parts[width:])
+        copies.append(
+            pltpu.make_async_copy(held_ref.at[:, here], out_ref.at[:, here], sems.at[i])
+        )
+        copies[i].start()
+    for copy in copies:
+        copy.wait()
 
 
 PARAMS = pltpu.CompilerParams(vmem_limit_bytes=12 << 20)
 VMEM = pl.BlockSpec(memory_space=pltpu.VMEM)
 HBM = pl.BlockSpec(memory_space=pltpu.HBM)
 SMEM = pl.BlockSpec(memory_space=pltpu.SMEM)
+ANY = pl.BlockSpec(memory_space=pl.ANY)
 
 
 def exchange(x, axis, groups):
@@ -374,7 +402,12 @@
             shape((1,), jnp.int32),
         ),
         in_specs=[VMEM] * 2,
-        out_specs=(VMEM, VMEM, SMEM),
+        out_specs=(ANY, VMEM, ANY),
+        scratch_shapes=[
+            pltpu.VMEM((width, cells), F32),
+            pltpu.SMEM((1,), jnp.int32),
+            pltpu.SemaphoreType.DMA((2,)),
+        ],
         compiler_params=PARAMS,
         name="merge_cells",
     )(got.reshape(place * (PLANES + 1), lanes), table)
@@ -392,11 +425,15 @@
     anomaly = pl.pallas_call(
         spread_kernel,
         out_shape=shape((width, patches), F32),
-        in_specs=[SMEM] + [VMEM] * 5,
-        out_specs=VMEM,
+        in_specs=[VMEM] * 5,
+        out_specs=ANY,
+        scratch_shapes=[
+            pltpu.VMEM((width, patches), F32),
+            pltpu.SemaphoreType.DMA((4,)),
+        ],
         compiler_params=PARAMS,
         name="spread_cells",
-    )(patch_count, back, first, second, cell_of, scaled)
+    )(back, first, second, cell_of, scaled)
     return merged, anomaly, full[0]
 
 

time: 84.1 us -> 83.9 us (level)
  no operation moved by 1% of the time
where the time goes in v7:
time: 83.9 us; the launch traced here: 82.9 us
  blocking collectives  75.8 us (90%)
  Pallas kernels  5.23 us (6%)
  between operations  1.31 us (2%)
    all_to_all x4, blocking collectives, exchange(): lax.all_to_all(x, axis, split_axis=0, concat_axis=0, tiled=True, axis_ind...  75.8 us
    pallas_call x1, Pallas kernels, pipeline(): pl.pallas_call(functools.partial(gather_kernel, devices), out_shape=(shap...  2.12 us

profile of v7, /device:TPU:1, one launch (start us, length us, event | category | flops | bytes accessed | tf_op | source)
XLA Modules:
  0.0 82.9 jit_solution(8626253560918821539)
XLA Ops:
  1.3 2.1 %gather_cells.3 = (f32[272,128]{1,0:T(8,128)S(1)}, f32[65,128]{1,0:T(8,128)S(1)}, f32[64,1024]{1,0:T(8,128)S(1)}, bf16[128,1024]{1,0:T(8,128)(2,1)S(1)}, bf16[25...) custom-call(s32[1]{0:T(128)S(6)} %copy.33.count_ref, f32[64,1024]{1,0:T(8,128)} %bitcast.48, s32[1,1024]{1,0:T(1,128)} %pft_ref.1, ...), custom_call_target="tpu_custom_call" | custom-call | tf_op jit(solution)/shard_map/gather_cells/pallas_call | solution.py:339
  3.4 27.6 %all_to_all.39 = f32[16,1,2176]{2,1,0:T(1,128)S(1)} all-to-all(f32[16,1,2176]{2,1,0:T(1,128)S(1)} %bitcast.47), channel_id=1, replica_groups={{0,32,64,96,128,160,192,224,256,288,320,352,384,416,448,480},{4,36,68,1..., dimensions={0} | all-to-all | bytes 278528 | tf_op jit(solution)/shard_map/all_to_all | solution.py:309
  31.0 0.3 turn_rows.3
  31.2 19.8 %all_to_all.40 = f32[32,1,2176]{2,1,0:T(1,128)S(1)} all-to-all(f32[32,1,2176]{2,1,0:T(1,128)S(1)} %bitcast.42), channel_id=1, replica_groups={{0,1,2,3,4,5,6,7,8,9,10,11,12,13,14,15,16,17,18,19,20,21,22,23,24,25,26..., dimensions={0} | all-to-all | bytes 557056 | tf_op jit(solution)/shard_map/all_to_all | solution.py:309
  51.0 1.4 %merge_cells.3 = (f32[64,128]{1,0:T(8,128)}, f32[512,128]{1,0:T(8,128)S(1)}, s32[1]{0:T(128)}) custom-call(f32[544,128]{1,0:T(8,128)S(1)} %bitcast.41, f32[65,128]{1,0:T(8,128)S(1)} %get-tuple-element.100.table_ref), custom_call_target="tpu_custom_call" | custom-call | tf_op jit(solution)/shard_map/merge_cells/pallas_call | solution.py:397
  52.4 12.8 %all_to_all.41 = f32[32,1,2048]{2,1,0:T(1,128)S(1)} all-to-all(f32[32,1,2048]{2,1,0:T(1,128)S(1)} %bitcast.46), channel_id=1, replica_groups={{0,1,2,3,4,5,6,7,8,9,10,11,12,13,14,15,16,17,18,19,20,21,22,23,24,25,26..., dimensions={0} | all-to-all | bytes 524288 | tf_op jit(solution)/shard_map/all_to_all | solution.py:309
  65.2 0.2 turn_back.3
  65.5 15.6 %all_to_all.42 = f32[16,1,2048]{2,1,0:T(1,128)S(1)} all-to-all(f32[16,1,2048]{2,1,0:T(1,128)S(1)} %bitcast.44), channel_id=1, replica_groups={{0,32,64,96,128,160,192,224,256,288,320,352,384,416,448,480},{4,36,68,1..., dimensions={0} | all-to-all | bytes 262144 | tf_op jit(solution)/shard_map/all_to_all | solution.py:309
  81.1 1.2 %spread_cells.3 = f32[64,1024]{1,0:T(8,128)} custom-call(f32[256,128]{1,0:T(8,128)S(1)} %bitcast.45, bf16[256,128]{1,0:T(8,128)(2,1)S(1)} %get-tuple-element.103.first_ref, bf16[256,128]{1,0:T(8,128)(2,1)S(1)} %get-tuple-element.104.second_ref, bf16[128,1024]{1,0:T(8,128)(2,1)S(1)} %get-tuple-element.105.cell_of_ref, ...), custom_call_target="tpu_custom_call" | custom-call | tf_op jit(solution)/shard_map/spread_cells/pallas_call | solution.py:425
  82.3 0.6 while.11

commit v8 on v7

--- a/solution.py
+++ b/solution.py
@@ -245,20 +245,15 @@
         )
 
 
-def merge_kernel(got_ref, table_ref, merged_ref, reply_ref, full_ref, held_ref, flag_ref, sems):
-    width, cells = held_ref.shape
+def merge_kernel(got_ref, table_ref, merged_ref, reply_ref, full_ref):
+    width, cells = merged_ref.shape
     devices = reply_ref.shape[0]
     place = devices // PLANES
     rows = jnp.concatenate(
         [got_ref[pl.ds(z, place, PLANES + 1), :] for z in range(PLANES)], axis=0
     )
     slots = got_ref[pl.ds(PLANES, place, PLANES + 1), :].astype(jnp.int32) - 1
-    flag_ref[0] = jnp.max(slots[:, slots.shape[1] - 1 :]) + 1
-    copies = (
-        pltpu.make_async_copy(flag_ref, full_ref, sems.at[0]),
-        pltpu.make_async_copy(held_ref, merged_ref, sems.at[1]),
-    )
-    copies[0].start()
+    full_ref[...] = jnp.broadcast_to(jnp.max(slots, axis=0, keepdims=True), full_ref.shape)
     lane = iota((place, cells), 1)
     first, second = (
         jnp.concatenate(
@@ -268,20 +263,31 @@
     )
     field, frac = table_ref[:width, :], table_ref[width:, :]
     merged = frac * from_rows(rows, first, second) + (1.0 - frac) * field
-    held_ref[...] = merged
-    copies[1].start()
+    merged_ref[...] = merged
     masks = jnp.concatenate([first, first, second, second], axis=1)
     rows = contract(masks, side_by_side(merged), 1, 1)
     for z in range(PLANES):
         reply_ref[pl.ds(z, place, PLANES), :] = rows[z * place : (z + 1) * place]
-    for copy in copies:
-        copy.wait()
 
 
 def spread_kernel(
-    back_ref, first_ref, second_ref, cell_of_ref, scaled_ref, out_ref, held_ref, sems
+    back_ref,
+    first_ref,
+    second_ref,
+    cell_of_ref,
+    scaled_ref,
+    mine_ref,
+    notes_ref,
+    out_ref,
+    merged_ref,
+    full_ref,
+    held_ref,
+    flag_ref,
+    sems,
 ):
     width, patches = scaled_ref.shape
+    kept = pltpu.make_async_copy(mine_ref, merged_ref, sems.at[4])
+    kept.start()
     merged = from_rows(back_ref[...], first_ref[...], second_ref[...])
     both = jnp.concatenate(pieces(merged, 2), axis=0)
     chunk = patches // 4
@@ -294,7 +300,11 @@
             pltpu.make_async_copy(held_ref.at[:, here], out_ref.at[:, here], sems.at[i])
         )
         copies[i].start()
-    for copy in copies:
+    notes = notes_ref[...]
+    flag_ref[0] = jnp.max(notes[:, notes.shape[1] - 1 :]) + 1
+    told = pltpu.make_async_copy(flag_ref, full_ref, sems.at[5])
+    told.start()
+    for copy in copies + [kept, told]:
         copy.wait()
 
 
@@ -394,20 +404,15 @@
         name="turn_rows",
     )(noted)
     got = exchange(send.reshape(place, 1, (PLANES + 1) * lanes), AXES, across)
-    merged, reply, full = pl.pallas_call(
+    mine, reply, notes = pl.pallas_call(
         merge_kernel,
         out_shape=(
             shape((width, cells), F32),
             shape((devices, lanes), F32),
-            shape((1,), jnp.int32),
+            shape((8, lanes), jnp.int32),
         ),
         in_specs=[VMEM] * 2,
-        out_specs=(ANY, VMEM, ANY),
-        scratch_shapes=[
-            pltpu.VMEM((width, cells), F32),
-            pltpu.SMEM((1,), jnp.int32),
-            pltpu.SemaphoreType.DMA((2,)),
-        ],
+        out_specs=(VMEM, VMEM, VMEM),
         compiler_params=PARAMS,
         name="merge_cells",
     )(got.reshape(place * (PLANES + 1), lanes), table)
@@ -422,18 +427,23 @@
     )(noted, back.reshape(devices, lanes))
     back = exchange(back.reshape(PLANES, 1, room * lanes), "clump", along)
     back = back.reshape(PLANES * room, lanes)
-    anomaly = pl.pallas_call(
+    anomaly, merged, full = pl.pallas_call(
         spread_kernel,
-        out_shape=shape((width, patches), F32),
-        in_specs=[VMEM] * 5,
-        out_specs=ANY,
+        out_shape=(
+            shape((width, patches), F32),
+            shape((width, cells), F32),
+            shape((1,), jnp.int32),
+        ),
+        in_specs=[VMEM] * 7,
+        out_specs=(ANY, ANY, ANY),
         scratch_shapes=[
             pltpu.VMEM((width, patches), F32),
-            pltpu.SemaphoreType.DMA((4,)),
+            pltpu.SMEM((1,), jnp.int32),
+            pltpu.SemaphoreType.DMA((6,)),
         ],
         compiler_params=PARAMS,
         name="spread_cells",
-    )(back, first, second, cell_of, scaled)
+    )(back, first, second, cell_of, scaled, mine, notes)
     return merged, anomaly, full[0]
 
 

time: 83.9 us -> 83.6 us (level)
  no operation moved by 1% of the time
where the time goes in v8:
time: 83.6 us; the launch traced here: 82.5 us
  blocking collectives  75.8 us (91%)
  Pallas kernels  4.79 us (6%)
  between operations  1.31 us (2%)
    all_to_all x4, blocking collectives, exchange(): lax.all_to_all(x, axis, split_axis=0, concat_axis=0, tiled=True, axis_ind...  75.8 us
    pallas_call x1, Pallas kernels, pipeline(): pl.pallas_call(functools.partial(gather_kernel, devices), out_shape=(shap...  2.12 us

profile of v8, /device:TPU:1, one launch (start us, length us, event | category | flops | bytes accessed | tf_op | source)
XLA Modules:
  0.0 82.5 jit_solution(3808616460971118545)
XLA Ops:
  1.3 2.1 %gather_cells.3 = (f32[272,128]{1,0:T(8,128)S(1)}, f32[65,128]{1,0:T(8,128)S(1)}, f32[64,1024]{1,0:T(8,128)S(1)}, bf16[128,1024]{1,0:T(8,128)(2,1)S(1)}, bf16[25...) custom-call(s32[1]{0:T(128)S(6)} %copy.33.count_ref, f32[64,1024]{1,0:T(8,128)} %bitcast.48, s32[1,1024]{1,0:T(1,128)} %pft_ref.1, ...), custom_call_target="tpu_custom_call" | custom-call | tf_op jit(solution)/shard_map/gather_cells/pallas_call | solution.py:349
  3.4 27.6 %all_to_all.39 = f32[16,1,2176]{2,1,0:T(1,128)S(1)} all-to-all(f32[16,1,2176]{2,1,0:T(1,128)S(1)} %bitcast.47), channel_id=1, replica_groups={{0,32,64,96,128,160,192,224,256,288,320,352,384,416,448,480},{4,36,68,1..., dimensions={0} | all-to-all | bytes 278528 | tf_op jit(solution)/shard_map/all_to_all | solution.py:319
  31.0 0.3 turn_rows.3
  31.2 19.8 %all_to_all.40 = f32[32,1,2176]{2,1,0:T(1,128)S(1)} all-to-all(f32[32,1,2176]{2,1,0:T(1,128)S(1)} %bitcast.42), channel_id=1, replica_groups={{0,1,2,3,4,5,6,7,8,9,10,11,12,13,14,15,16,17,18,19,20,21,22,23,24,25,26..., dimensions={0} | all-to-all | bytes 557056 | tf_op jit(solution)/shard_map/all_to_all | solution.py:319
  51.0 0.9 %merge_cells.3 = (f32[64,128]{1,0:T(8,128)S(1)}, f32[512,128]{1,0:T(8,128)S(1)}, s32[8,128]{1,0:T(8,128)S(1)}) custom-call(f32[544,128]{1,0:T(8,128)S(1)} %bitcast.41, f32[65,128]{1,0:T(8,128)S(1)} %get-tuple-element.106.table_ref), custom_call_target="tpu_custom_call" | custom-call | tf_op jit(solution)/shard_map/merge_cells/pallas_call | solution.py:407
  51.9 12.8 %all_to_all.41 = f32[32,1,2048]{2,1,0:T(1,128)S(1)} all-to-all(f32[32,1,2048]{2,1,0:T(1,128)S(1)} %bitcast.46), channel_id=1, replica_groups={{0,1,2,3,4,5,6,7,8,9,10,11,12,13,14,15,16,17,18,19,20,21,22,23,24,25,26..., dimensions={0} | all-to-all | bytes 524288 | tf_op jit(solution)/shard_map/all_to_all | solution.py:319
  64.7 0.2 turn_back.3
  65.0 15.7 %all_to_all.42 = f32[16,1,2048]{2,1,0:T(1,128)S(1)} all-to-all(f32[16,1,2048]{2,1,0:T(1,128)S(1)} %bitcast.45), channel_id=1, replica_groups={{0,32,64,96,128,160,192,224,256,288,320,352,384,416,448,480},{4,36,68,1..., dimensions={0} | all-to-all | bytes 262144 | tf_op jit(solution)/shard_map/all_to_all | solution.py:319
  80.6 1.2 %spread_cells.3 = (f32[64,1024]{1,0:T(8,128)}, f32[64,128]{1,0:T(8,128)}, s32[1]{0:T(128)}) custom-call(f32[256,128]{1,0:T(8,128)S(1)} %bitcast.44, bf16[256,128]{1,0:T(8,128)(2,1)S(1)} %get-tuple-element.108.first_ref, bf16[256,128]{1,0:T(8,128)(2,1)S(1)} %get-tuple-element.109.second_ref, bf16[128,1024]{1,0:T(8,128)(2,1)S(1)} %get-tuple-element.110.cell_of_ref, ...), custom_call_target="tpu_custom_call" | custom-call | tf_op jit(solution)/shard_map/spread_cells/pallas_call | solution.py:430
  81.9 0.6 while.11

commit v9 on v8

--- a/solution.py
+++ b/solution.py
@@ -456,7 +456,7 @@
         return merged, anomaly, jnp.int32(0)
 
     merged, anomaly, _ = lax.while_loop(
-        lambda state: state[2] > 0, again, pipeline(most // 2, *args)
+        lambda state: state[2] > 0, again, pipeline(most * 15 // 32, *args)
     )
     return merged.T, anomaly.T[None]
 

time: 83.6 us -> 83.1 us (level)
  no operation moved by 1% of the time
where the time goes in v9:
time: 83.1 us; the launch traced here: 82.1 us
  blocking collectives  75.4 us (91%)
  Pallas kernels  4.81 us (6%)
  between operations  1.3 us (2%)
    all_to_all x4, blocking collectives, exchange(): lax.all_to_all(x, axis, split_axis=0, concat_axis=0, tiled=True, axis_ind...  75.4 us
    pallas_call x1, Pallas kernels, pipeline(): pl.pallas_call(functools.partial(gather_kernel, devices), out_shape=(shap...  2.11 us

profile of v9, /device:TPU:1, one launch (start us, length us, event | category | flops | bytes accessed | tf_op | source)
XLA Modules:
  0.0 82.1 jit_solution(17727894471961432812)
XLA Ops:
  1.3 2.1 %gather_cells.3 = (f32[256,128]{1,0:T(8,128)S(1)}, f32[65,128]{1,0:T(8,128)S(1)}, f32[64,1024]{1,0:T(8,128)S(1)}, bf16[128,1024]{1,0:T(8,128)(2,1)S(1)}, bf16[24...) custom-call(s32[1]{0:T(128)S(6)} %copy.33.count_ref, f32[64,1024]{1,0:T(8,128)} %bitcast.48, s32[1,1024]{1,0:T(1,128)} %pft_ref.1, ...), custom_call_target="tpu_custom_call" | custom-call | tf_op jit(solution)/shard_map/gather_cells/pallas_call | solution.py:349
  3.4 27.5 %all_to_all.39 = f32[16,1,2048]{2,1,0:T(1,128)S(1)} all-to-all(f32[16,1,2048]{2,1,0:T(1,128)S(1)} %bitcast.47), channel_id=1, replica_groups={{0,32,64,96,128,160,192,224,256,288,320,352,384,416,448,480},{4,36,68,1..., dimensions={0} | all-to-all | bytes 262144 | tf_op jit(solution)/shard_map/all_to_all | solution.py:319
  30.9 0.3 turn_rows.3
  31.2 19.7 %all_to_all.40 = f32[32,1,2176]{2,1,0:T(1,128)S(1)} all-to-all(f32[32,1,2176]{2,1,0:T(1,128)S(1)} %bitcast.42), channel_id=1, replica_groups={{0,1,2,3,4,5,6,7,8,9,10,11,12,13,14,15,16,17,18,19,20,21,22,23,24,25,26..., dimensions={0} | all-to-all | bytes 557056 | tf_op jit(solution)/shard_map/all_to_all | solution.py:319
  50.9 0.9 %merge_cells.3 = (f32[64,128]{1,0:T(8,128)S(1)}, f32[512,128]{1,0:T(8,128)S(1)}, s32[8,128]{1,0:T(8,128)S(1)}) custom-call(f32[544,128]{1,0:T(8,128)S(1)} %bitcast.41, f32[65,128]{1,0:T(8,128)S(1)} %get-tuple-element.106.table_ref), custom_call_target="tpu_custom_call" | custom-call | tf_op jit(solution)/shard_map/merge_cells/pallas_call | solution.py:407
  51.8 12.8 %all_to_all.41 = f32[32,1,2048]{2,1,0:T(1,128)S(1)} all-to-all(f32[32,1,2048]{2,1,0:T(1,128)S(1)} %bitcast.46), channel_id=1, replica_groups={{0,1,2,3,4,5,6,7,8,9,10,11,12,13,14,15,16,17,18,19,20,21,22,23,24,25,26..., dimensions={0} | all-to-all | bytes 524288 | tf_op jit(solution)/shard_map/all_to_all | solution.py:319
  64.6 0.2 turn_back.3
  64.9 15.4 %all_to_all.42 = f32[16,1,1920]{2,1,0:T(1,128)S(1)} all-to-all(f32[16,1,1920]{2,1,0:T(1,128)S(1)} %bitcast.45), channel_id=1, replica_groups={{0,32,64,96,128,160,192,224,256,288,320,352,384,416,448,480},{4,36,68,1..., dimensions={0} | all-to-all | bytes 245760 | tf_op jit(solution)/shard_map/all_to_all | solution.py:319
  80.3 1.2 %spread_cells.3 = (f32[64,1024]{1,0:T(8,128)}, f32[64,128]{1,0:T(8,128)}, s32[1]{0:T(128)}) custom-call(f32[240,128]{1,0:T(8,128)S(1)} %bitcast.44, bf16[240,128]{1,0:T(8,128)(2,1)S(1)} %get-tuple-element.108.first_ref, bf16[240,128]{1,0:T(8,128)(2,1)S(1)} %get-tuple-element.109.second_ref, bf16[128,1024]{1,0:T(8,128)(2,1)S(1)} %get-tuple-element.110.cell_of_ref, ...), custom_call_target="tpu_custom_call" | custom-call | tf_op jit(solution)/shard_map/spread_cells/pallas_call | solution.py:430
  81.5 0.6 while.11

commit v10 on v9

--- a/solution.py
+++ b/solution.py
@@ -451,12 +451,14 @@
     devices = lax.axis_size("clump") * lax.axis_size("grp")
     most = devices // PLANES
 
-    def again(state):
-        merged, anomaly, _ = pipeline(most, *args)
-        return merged, anomaly, jnp.int32(0)
-
-    merged, anomaly, _ = lax.while_loop(
-        lambda state: state[2] > 0, again, pipeline(most * 15 // 32, *args)
+    merged, anomaly, full = pipeline(most * 15 // 32, *args)
+    merged, anomaly, full, args = lax.optimization_barrier((merged, anomaly, full, args))
+    merged, anomaly = lax.cond(
+        full > 0,
+        lambda held, given: pipeline(most, *given)[:2],
+        lambda held, given: held,
+        (merged, anomaly),
+        args,
     )
     return merged.T, anomaly.T[None]
 

time: 83.1 us -> 83.1 us (level)
  no operation moved by 1% of the time
where the time goes in v10:
time: 83.1 us; the launch traced here: 82.2 us
  blocking collectives  75.4 us (91%)
  Pallas kernels  4.81 us (6%)
  between operations  1.98 us (2%)
    all_to_all x4, blocking collectives, exchange(): lax.all_to_all(x, axis, split_axis=0, concat_axis=0, tiled=True, axis_ind...  75.4 us
    pallas_call x1, Pallas kernels, pipeline(): pl.pallas_call(functools.partial(gather_kernel, devices), out_shape=(shap...  2.11 us

profile of v10, /device:TPU:1, one launch (start us, length us, event | category | flops | bytes accessed | tf_op | source)
XLA Modules:
  0.0 82.2 jit_solution(8723525534566663690)
XLA Ops:
  1.3 2.1 %gather_cells.3 = (f32[256,128]{1,0:T(8,128)S(1)}, f32[65,128]{1,0:T(8,128)S(1)}, f32[64,1024]{1,0:T(8,128)S(1)}, bf16[128,1024]{1,0:T(8,128)(2,1)S(1)}, bf16[24...) custom-call(s32[1]{0:T(128)S(6)} %copy.27.count_ref, f32[64,1024]{1,0:T(8,128)} %bitcast.49, s32[1,1024]{1,0:T(1,128)} %pft_ref.1, ...), custom_call_target="tpu_custom_call" | custom-call | tf_op jit(solution)/shard_map/gather_cells/pallas_call | solution.py:349
  3.4 27.5 %all_to_all.40 = f32[16,1,2048]{2,1,0:T(1,128)S(1)} all-to-all(f32[16,1,2048]{2,1,0:T(1,128)S(1)} %bitcast.48), channel_id=1, replica_groups={{0,32,64,96,128,160,192,224,256,288,320,352,384,416,448,480},{4,36,68,1..., dimensions={0} | all-to-all | bytes 262144 | tf_op jit(solution)/shard_map/all_to_all | solution.py:319
  30.9 0.3 turn_rows.3
  31.2 19.7 %all_to_all.41 = f32[32,1,2176]{2,1,0:T(1,128)S(1)} all-to-all(f32[32,1,2176]{2,1,0:T(1,128)S(1)} %bitcast.37), channel_id=1, replica_groups={{0,1,2,3,4,5,6,7,8,9,10,11,12,13,14,15,16,17,18,19,20,21,22,23,24,25,26..., dimensions={0} | all-to-all | bytes 557056 | tf_op jit(solution)/shard_map/all_to_all | solution.py:319
  50.9 0.9 %merge_cells.3 = (f32[64,128]{1,0:T(8,128)S(1)}, f32[512,128]{1,0:T(8,128)S(1)}, s32[8,128]{1,0:T(8,128)S(1)}) custom-call(f32[544,128]{1,0:T(8,128)S(1)} %bitcast.35, f32[65,128]{1,0:T(8,128)S(1)} %get-tuple-element.87.table_ref), custom_call_target="tpu_custom_call" | custom-call | tf_op jit(solution)/shard_map/merge_cells/pallas_call | solution.py:407
  51.8 12.8 %all_to_all.42 = f32[32,1,2048]{2,1,0:T(1,128)S(1)} all-to-all(f32[32,1,2048]{2,1,0:T(1,128)S(1)} %bitcast.46), channel_id=1, replica_groups={{0,1,2,3,4,5,6,7,8,9,10,11,12,13,14,15,16,17,18,19,20,21,22,23,24,25,26..., dimensions={0} | all-to-all | bytes 524288 | tf_op jit(solution)/shard_map/all_to_all | solution.py:319
  64.6 0.2 turn_back.3
  64.9 15.4 %all_to_all.43 = f32[16,1,1920]{2,1,0:T(1,128)S(1)} all-to-all(f32[16,1,1920]{2,1,0:T(1,128)S(1)} %bitcast.44), channel_id=1, replica_groups={{0,32,64,96,128,160,192,224,256,288,320,352,384,416,448,480},{4,36,68,1..., dimensions={0} | all-to-all | bytes 245760 | tf_op jit(solution)/shard_map/all_to_all | solution.py:319
  80.3 1.2 %spread_cells.3 = (f32[64,1024]{1,0:T(8,128)}, f32[64,128]{1,0:T(8,128)}, s32[1]{0:T(128)}) custom-call(f32[240,128]{1,0:T(8,128)S(1)} %bitcast.43, bf16[240,128]{1,0:T(8,128)(2,1)S(1)} %get-tuple-element.89.first_ref, bf16[240,128]{1,0:T(8,128)(2,1)S(1)} %get-tuple-element.90.second_ref, bf16[128,1024]{1,0:T(8,128)(2,1)S(1)} %get-tuple-element.91.cell_of_ref, ...), custom_call_target="tpu_custom_call" | custom-call | tf_op jit(solution)/shard_map/spread_cells/pallas_call | solution.py:430
  (1 shorter events, 0.0 us)
